TPU v7x, 256 devices: a whole 4x4x8 slice. The times are simulated.
256 devices in a mesh: seq: 64 (over z_hi, x, y), heads: 4 (over z_lo, core).
Axes of the slice: x: 4, y: 4, z: 8 (z_hi: 4, z_lo: 2; z = z_hi * 2 + z_lo), core: 2. Of those that a mesh axis runs over, the one named last changes fastest.
Arguments:
- queries: bfloat16 [16384, 16, 128], P('seq', 'heads'), may hold values from -6 to 6
- key_vecs: bfloat16 [16384, 16, 128], P('seq', 'heads'), may hold values from -12 to 12
- values: bfloat16 [16384, 32, 128], P('seq', 'heads'), may hold values from -6 to 6
- strength: float32 [16384, 32], P('seq', 'heads'), may hold values from 0 to 1, as said below
- decay_rate: float32 [16384, 32], P('seq', 'heads'), may hold values from 0 to 0.15, as said below
- norm_gain: float32 [128], replicated, may hold values from 0.5 to 1.5
- w_out: bfloat16 [4096, 2048], P('heads'), may hold values from -0.09375 to 0.09375
Outputs:
- mixed: bfloat16 [16384, 2048], P(('seq', 'heads'))
Inputs may be any that keep to these rules, and one draw needn't show every extreme that they name: Every write strength lies strictly between 0 and 1. `decay_rate`: every decay rate is positive.
All inputs are finite; a program needn't handle non-finite values.
Results may differ from a plain program's by a relative error of at most 0.0049.
Values sent between devices are 32-bit elements; how exact they have to be, the bound alone decides.
A program may use at most 192 MiB of HBM per device.

v0:
```python
import jax
import jax.numpy as jnp
from jax import lax
from jax.sharding import Mesh
from jax.sharding import PartitionSpec as P

BLOCK_TOKENS = 64
SEQ = ("seq_0", "seq_1", "seq_2")
SEQ_HEADS = ("seq_0", "seq_1", "seq_2", "heads")


strict_precision = lax.Precision.HIGHEST
norm_eps = 1e-12
unit_eps = 1e-06


def neutral_like(x, identity):
    return jax.tree.map(
        lambda part, zero: jnp.zeros_like(part) + jnp.asarray(zero, part.dtype), x, identity
    )


def prefix_by_axis(x, axes, combine, identity):
    before = start = neutral_like(x, identity)
    running = x
    for axis in reversed(axes):
        devices, place = (lax.axis_size(axis), lax.axis_index(axis))
        pieces = jax.tree.map(lambda part: lax.all_gather(part, axis), running)
        inside, running = (start, start)
        for k in range(devices):
            passed = k < place
            running = combine(running, jax.tree.map(lambda part: part[k], pieces))
            inside = jax.tree.map(lambda new, old: jnp.where(passed, new, old), running, inside)
        before = combine(inside, before)
    return before


def split_up(x, dim, devices):
    shape = x.shape
    tiles = x.reshape(*shape[:dim], devices, shape[dim] // devices, *shape[dim + 1 :])
    return jnp.moveaxis(tiles, dim, 0)


def sum_at_owner(x, axis, dim):
    devices = lax.axis_size(axis)
    tiles = lax.all_to_all(split_up(x, dim, devices), axis, 0, 0, tiled=True)
    return jnp.sum(tiles, axis=0)


def unit_rows(matrix):
    matrix = matrix.astype(jnp.float32)
    return matrix / jnp.sqrt(jnp.sum(matrix * matrix, axis=-1, keepdims=True) + unit_eps)


def prepare(query_blk, key_blk, value_blk, strength_blk, decay_blk):
    group_size = value_blk.shape[1] // query_blk.shape[1]
    normalized_queries = jnp.repeat(
        jnp.transpose(unit_rows(query_blk), (1, 0, 2)), group_size, axis=0
    )
    keys_n = jnp.repeat(jnp.transpose(unit_rows(key_blk), (1, 0, 2)), group_size, axis=0)
    values_f = jnp.transpose(value_blk.astype(jnp.float32), (1, 0, 2))
    writes = jnp.transpose(strength_blk)
    decay_logarithm = -jnp.cumsum(jnp.transpose(decay_blk), axis=1)
    return (normalized_queries, keys_n, values_f, writes, decay_logarithm)


def block_parts(normalized_queries, keys_n, values_f, writes, decay_logarithm):
    key_width = keys_n.shape[2]
    length = keys_n.shape[1]
    row_ids = lax.broadcasted_iota(jnp.int32, (length, length), 0)
    col_ids = lax.broadcasted_iota(jnp.int32, (length, length), 1)
    ratios = jnp.exp(jnp.minimum(decay_logarithm[:, :, None] - decay_logarithm[:, None, :], 0.0))
    key_dots = jnp.einsum("hik,hjk->hij", keys_n, keys_n, precision=strict_precision)
    query_dots = jnp.einsum("hik,hjk->hij", normalized_queries, keys_n, precision=strict_precision)
    system = jnp.where(row_ids > col_ids, writes[:, :, None] * ratios * key_dots, 0.0)
    system = system + jnp.eye(length, dtype=jnp.float32)
    scaled = writes * jnp.exp(decay_logarithm)
    right_side = jnp.concatenate(
        [scaled[:, :, None] * keys_n, writes[:, :, None] * values_f], axis=2
    )
    solved = jax.scipy.linalg.solve_triangular(system, right_side, lower=True, unit_diagonal=True)
    weighted_key_rows = solved[:, :, :key_width]
    corrected_values = solved[:, :, key_width:]
    mixing = jnp.where(row_ids >= col_ids, ratios * query_dots, 0.0)
    trailing_keys = jnp.exp(decay_logarithm[:, -1:] - decay_logarithm)[:, :, None] * keys_n
    return (weighted_key_rows, corrected_values, mixing, trailing_keys)


def block_apply(
    memory_state,
    normalized_queries,
    decay_logarithm,
    weighted_key_rows,
    corrected_values,
    mixing,
    trailing_keys,
):
    state_increment = corrected_values - jnp.einsum(
        "qjl,qlo->qjo", weighted_key_rows, memory_state, precision=strict_precision
    )
    output_rows = jnp.exp(decay_logarithm)[:, :, None] * jnp.einsum(
        "qjl,qlo->qjo", normalized_queries, memory_state, precision=strict_precision
    )
    output_rows = output_rows + jnp.einsum(
        "hij,hjv->hiv", mixing, state_increment, precision=strict_precision
    )
    updated_state = jnp.exp(decay_logarithm[:, -1])[:, None, None] * memory_state
    updated_state = updated_state + jnp.einsum(
        "oqm,oqy->omy", trailing_keys, state_increment, precision=strict_precision
    )
    return (updated_state, output_rows)


def normalize(output_rows, norm_gain):
    mean_sq = jnp.mean(output_rows * output_rows, axis=-1, keepdims=True)
    return (output_rows / jnp.sqrt(mean_sq + norm_eps) * norm_gain).astype(jnp.bfloat16)


def compose_maps(transit_all, offset_all):

    def fold_maps(carried, map_pair):
        transit, block_displacement = map_pair
        matrix = jnp.einsum("hij,hjk->hik", transit, carried[0], precision=strict_precision)
        shifted = (
            jnp.einsum("hij,hjv->hiv", transit, carried[1], precision=strict_precision)
            + block_displacement
        )
        return ((matrix, shifted), None)

    first_shape = transit_all.shape[1:]
    initial = (
        jnp.broadcast_to(jnp.eye(first_shape[1], dtype=jnp.float32), first_shape),
        jnp.zeros(offset_all.shape[1:], jnp.float32),
    )
    result, _ = lax.scan(fold_maps, initial, (transit_all, offset_all))
    return result


def chain_maps(earlier_map, later_map):
    matrix = jnp.einsum("hij,hjk->hik", later_map[0], earlier_map[0], precision=strict_precision)
    shifted = (
        jnp.einsum("hij,hjv->hiv", later_map[0], earlier_map[1], precision=strict_precision)
        + later_map[1]
    )
    return (matrix, shifted)


def identity_of(composed):
    return (
        jnp.broadcast_to(jnp.eye(composed[0].shape[1], dtype=jnp.float32), composed[0].shape),
        jnp.zeros_like(composed[1]),
    )


def body(queries, key_vecs, values, strength, decay_rate, norm_gain, w_out):
    local_len = queries.shape[0]
    block_count = local_len // BLOCK_TOKENS
    heads_v = values.shape[1]
    key_width = key_vecs.shape[2]
    value_width = values.shape[2]
    blocks = (
        queries.reshape(block_count, BLOCK_TOKENS, queries.shape[1], key_width),
        key_vecs.reshape(block_count, BLOCK_TOKENS, key_vecs.shape[1], key_width),
        values.reshape(block_count, BLOCK_TOKENS, heads_v, value_width),
        strength.reshape(block_count, BLOCK_TOKENS, heads_v),
        decay_rate.reshape(block_count, BLOCK_TOKENS, heads_v),
    )

    def analyse(carried, pieces):
        prepared = prepare(pieces[0], pieces[1], pieces[2], pieces[3], pieces[4])
        weighted_key_rows, corrected_values, mixing, trailing_keys = block_parts(*prepared)
        block_decay = jnp.exp(prepared[4][:, -1])
        transit = block_decay[:, None, None] * jnp.eye(key_width, dtype=jnp.float32)
        transit = transit - jnp.einsum(
            "hck,hcj->hkj", trailing_keys, weighted_key_rows, precision=strict_precision
        )
        block_displacement = jnp.einsum(
            "oqm,oqy->omy", trailing_keys, corrected_values, precision=strict_precision
        )
        stored = (
            prepared[0],
            prepared[4],
            weighted_key_rows,
            corrected_values,
            mixing,
            trailing_keys,
        )
        return (carried, (stored, (transit, block_displacement)))

    _, (stored_all, map_pairs) = lax.scan(analyse, jnp.zeros((), jnp.float32), blocks)
    transit_all, offset_all = map_pairs
    composed = compose_maps(transit_all, offset_all)
    earlier = prefix_by_axis(composed, SEQ, chain_maps, identity_of(composed))
    incoming = earlier[1]

    def emit(memory_state, stored):
        updated_state, output_rows = block_apply(
            memory_state, stored[0], stored[1], stored[2], stored[3], stored[4], stored[5]
        )
        return (updated_state, normalize(jnp.transpose(output_rows, (1, 0, 2)), norm_gain))

    _, normed = lax.scan(emit, incoming, stored_all)
    flat = normed.reshape(local_len, heads_v * value_width)
    mixed = sum_at_owner(jnp.dot(flat, w_out, preferred_element_type=jnp.float32), "heads", 0)
    return mixed.astype(jnp.bfloat16)


def solution(mesh):
    finer = Mesh(
        mesh.devices.reshape(4, 4, 4, mesh.shape["heads"]), ("seq_0", "seq_1", "seq_2", "heads")
    )
    placed = (
        P(SEQ, "heads", None),
        P(SEQ, "heads", None),
        P(SEQ, "heads", None),
        P(SEQ, "heads"),
        P(SEQ, "heads"),
        P(),
        P("heads", None),
    )
    return jax.shard_map(
        body, mesh=finer, in_specs=placed, out_specs=P(SEQ_HEADS, None), check_vma=False
    )
```

profile of v0, /device:TPU:192, one launch (start us, length us, event | category | flops | bytes accessed | tf_op | source)
XLA Modules:
  0.0 562.8 jit_solution(2411839015668569248)
XLA Ops:
  8.1 214.4 %while.49 = (s32[]{:T(128)}, f32[4,8,64,128]{3,2,1,0:T(8,128)}, f32[4,8,64]{2,1,0:T(8,128)S(1)}, f32[4,8,64,128]{3,2,1,0:T(8,128)}, f32[4,8,64,128]{3,2,1,0:T(8,...) while((s32[]{:T(128)}, f32[4,8,64,128]{3,2,1,0:T(8,128)}, ...), condition=%wide.region_4.5_spmd, body=%wide.region_0.4_spmd.sunk | while | flops 404191296 | bytes 9727317 | solution.py:190
  10.1 1.3 fusion.225
  11.4 40.7 %custom-call.15 = f32[8,1,64,64]{2,3,1,0:T(8,128)} custom-call(f32[8,1,64,64]{3,2,1,0:T(8,128)} %fusion.225), custom_call_target="InvertDiagBlocksLowerTriangular" | custom-call | tf_op jit(solution)/shard_map/while/body/eval_jaxpr/jit(_solve_triangular)/vmap()/triangular_solve | solution.py:81
  53.1 1.6 fusion.226
  54.7 1.0 bitcast_dynamic-update-slice_fusion.9
  56.8 1.8 fusion.230
  59.8 1.3 fusion.227
  63.8 1.3 fusion.225
  65.0 40.7 %custom-call.15 = f32[8,1,64,64]{2,3,1,0:T(8,128)} custom-call(f32[8,1,64,64]{3,2,1,0:T(8,128)} %fusion.225), custom_call_target="InvertDiagBlocksLowerTriangular" | custom-call | tf_op jit(solution)/shard_map/while/body/eval_jaxpr/jit(_solve_triangular)/vmap()/triangular_solve | solution.py:81
  106.8 1.6 fusion.226
  110.4 1.8 fusion.230
  113.4 1.3 fusion.227
  117.4 1.3 fusion.225
  118.7 40.7 %custom-call.15 = f32[8,1,64,64]{2,3,1,0:T(8,128)} custom-call(f32[8,1,64,64]{3,2,1,0:T(8,128)} %fusion.225), custom_call_target="InvertDiagBlocksLowerTriangular" | custom-call | tf_op jit(solution)/shard_map/while/body/eval_jaxpr/jit(_solve_triangular)/vmap()/triangular_solve | solution.py:81
  160.4 1.6 fusion.226
  164.0 1.8 fusion.230
  167.0 1.3 fusion.227
  171.0 1.3 fusion.225
  172.3 40.7 %custom-call.15 = f32[8,1,64,64]{2,3,1,0:T(8,128)} custom-call(f32[8,1,64,64]{3,2,1,0:T(8,128)} %fusion.225), custom_call_target="InvertDiagBlocksLowerTriangular" | custom-call | tf_op jit(solution)/shard_map/while/body/eval_jaxpr/jit(_solve_triangular)/vmap()/triangular_solve | solution.py:81
  214.0 1.6 fusion.226
  217.6 1.8 fusion.230
  220.6 1.3 fusion.227
  222.6 9.9 %while.51 = (s32[]{:T(128)}, f32[8,128,128]{2,1,0:T(8,128)S(1)}, f32[8,128,128]{2,1,0:T(8,128)S(1)}, f32[4,8,128,128]{3,2,1,0:T(8,128)S(1)}, f32[4,8,128,128]{3,2,1,0:T(8,128)}, /*index=5*/s32[]{:T(128)}, s32[]{:T(128)}) while((s32[]{:T(128)}, f32[8,128,128]{2,1,0:T(8,128)S(1)}, f32[8,128,128]{2,1,0:T(8,128)S(1)}, ...), condition=%wide.region_6.7_spmd.clone, body=%wide.region_5.6_spmd.clone.sunk | while | flops 402915328 | bytes 5768283 | solution.py:135
  222.7 1.7 convolution_add_fusion.18
  225.1 1.7 convolution_add_fusion.18
  227.6 1.7 convolution_add_fusion.18
  230.1 1.7 convolution_add_fusion.18
  234.1 33.5 %all-gather.13.cloned.1.call-done = f32[32,128,128]{2,1,0:T(8,128)} async-done(((f32[8,128,128]{2,1,0:T(8,128)}), f32[32,128,128]{2,1,0:T(8,128)}) %all-gather.13.cloned.1.call-update) | async-done | bytes 2097168 | tf_op jit(solution)/shard_map/all_gather | solution.py:28
  267.6 35.2 %all-gather.19.cloned.1.call-done = f32[32,128,128]{2,1,0:T(8,128)} async-done(((f32[8,128,128]{2,1,0:T(8,128)}), f32[32,128,128]{2,1,0:T(8,128)}) %all-gather.19.cloned.1.call-update) | async-done | bytes 2097168 | tf_op jit(solution)/shard_map/all_gather | solution.py:28
  302.8 1.8 convolution_add_fusion.11
  305.3 1.8 convolution_add_fusion.10
  307.8 1.5 convolution_add_fusion.8
  313.7 1.5 fusion.115
  315.5 27.4 %all-gather.21.cloned.1.call-done = f32[32,128,128]{2,1,0:T(8,128)} async-done(((f32[8,128,128]{2,1,0:T(8,128)}), f32[32,128,128]{2,1,0:T(8,128)}) %all-gather.21.cloned.1.call-update) | async-done | bytes 2097168 | tf_op jit(solution)/shard_map/all_gather | solution.py:28
  342.8 35.1 %all-gather.15.cloned.1.call-done = f32[32,128,128]{2,1,0:T(8,128)} async-done(((f32[8,128,128]{2,1,0:T(8,128)}), f32[32,128,128]{2,1,0:T(8,128)}) %all-gather.15.cloned.1.call-update) | async-done | bytes 2097168 | tf_op jit(solution)/shard_map/all_gather | solution.py:28
  377.9 1.9 convolution_add_fusion.12
  380.6 1.9 convolution_add_fusion.7
  384.1 1.5 convolution_add_fusion.5
  389.3 1.5 fusion.118
  392.3 1.5 fusion.63
  393.8 1.5 fusion.68
  395.3 40.3 %all-gather.23.cloned.1.call-done = f32[32,128,128]{2,1,0:T(8,128)} async-done(((f32[8,128,128]{2,1,0:T(8,128)}), f32[32,128,128]{2,1,0:T(8,128)}) %all-gather.23.cloned.1.call-update) | async-done | bytes 2097168 | tf_op jit(solution)/shard_map/all_gather | solution.py:28
  435.6 51.7 %all-gather.17.cloned.1.call-done = f32[32,128,128]{2,1,0:T(8,128)} async-done(((f32[8,128,128]{2,1,0:T(8,128)}), f32[32,128,128]{2,1,0:T(8,128)}) %all-gather.17.cloned.1.call-update) | async-done | bytes 2097168 | tf_op jit(solution)/shard_map/all_gather | solution.py:28
  487.3 1.9 convolution_add_fusion.13
  489.2 1.8 convolution_add_fusion.4
  494.5 28.8 %while.50 = (s32[]{:T(128)}, f32[8,128,128]{2,1,0:T(8,128)S(1)}, bf16[4,64,8,128]{3,2,1,0:T(8,128)(2,1)S(1)}, f32[4,8,64]{2,1,0:T(8,128)S(1)}, f32[4,8,64,128]{3...) while((s32[]{:T(128)}, f32[8,128,128]{2,1,0:T(8,128)S(1)}, ...), condition=%wide.region_9.10_spmd, body=%wide.region_7.9_spmd.sunk | while | flops 353108480 | bytes 5666005 | solution.py:202
  494.7 1.6 fusion.239
  496.2 1.6 convolution_subtract_fusion.3
  497.9 1.5 multiply_reduce_fusion.2
  499.6 2.1 convolution_add_fusion.17
  501.9 1.6 fusion.239
  503.4 1.6 convolution_subtract_fusion.3
  505.1 1.5 multiply_reduce_fusion.2
  506.8 2.1 convolution_add_fusion.17
  509.1 1.6 fusion.239
  510.6 1.6 convolution_subtract_fusion.3
  512.3 1.5 multiply_reduce_fusion.2
  514.0 2.1 convolution_add_fusion.17
  516.3 1.6 fusion.239
  517.8 1.6 convolution_subtract_fusion.3
  519.5 1.5 multiply_reduce_fusion.2
  521.2 2.1 convolution_add_fusion.17
  523.5 3.4 fusion.55
  527.0 28.1 %all_to_all.5 = f32[4,64,2048]{2,1,0:T(8,128)S(1)} all-to-all(f32[4,64,2048]{2,1,0:T(8,128)S(1)} %fusion.55), channel_id=1, replica_groups=mesh['seq_0'=4,'seq_1'=4,'seq_2'=4,'heads'=4] {'heads'}, dimensions={0} | all-to-all | bytes 4194304 | tf_op jit(solution)/shard_map/all_to_all | solution.py:46
  (272 shorter events, 52.0 us)
Async XLA Ops:
  6.5 261.0 %all-gather.13.cloned.1.call-start = ((), (), s32[]{:S(2)}) async-start(), calls=%async_computation.1 | async-start | bytes 2621440 | tf_op jit(solution)/shard_map/all_gather | solution.py:28
  232.5 0.8 copy-start.3
  232.5 1.0 copy-start.4
  233.3 69.5 %all-gather.19.cloned.1.call-start = ((), (), s32[]{:S(2)}) async-start(), calls=%async_computation.4 | async-start | bytes 2621440 | tf_op jit(solution)/shard_map/all_gather | solution.py:28
  234.0 108.8 %all-gather.21.cloned.1.call-start = ((), (), s32[]{:S(2)}) async-start(), calls=%async_computation.5 | async-start | bytes 2621440 | tf_op jit(solution)/shard_map/all_gather | solution.py:28
  267.6 37.8 %copy-start = (f32[32,128,128]{2,1,0:T(8,128)S(1)}, f32[32,128,128]{2,1,0:T(8,128)}, u32[]{:S(2)}) copy-start(f32[32,128,128]{2,1,0:T(8,128)} %all-gather.13.cloned.1.call-done) | copy-start | bytes 6291460
  304.6 0.8 copy-start.13
  305.3 1.8 copy-start.12
  309.3 68.5 %all-gather.15.cloned.1.call-start = ((), (), s32[]{:S(2)}) async-start(), calls=%async_computation.2 | async-start | bytes 2621440 | tf_op jit(solution)/shard_map/all_gather | solution.py:28
  310.0 0.8 copy-start.24
  311.4 0.8 copy-start.15
  312.9 0.8 copy-start.16
  315.2 120.4 %all-gather.23.cloned.1.call-start = ((), (), s32[]{:S(2)}) async-start(), calls=%async_computation.6 | async-start | bytes 2621440 | tf_op jit(solution)/shard_map/all_gather | solution.py:28
  377.9 2.7 copy-start.1
  379.8 0.8 copy-start.17
  380.6 1.9 copy-start.11
  382.5 0.8 copy-start.6
  383.3 0.8 copy-start.8
  385.6 101.7 %all-gather.17.cloned.1.call-start = ((), (), s32[]{:S(2)}) async-start(), calls=%async_computation.3 | async-start | bytes 2621440 | tf_op jit(solution)/shard_map/all_gather | solution.py:28
  386.2 0.8 copy-start.25
  387.7 0.8 copy-start.19
  388.5 0.8 copy-start.21
  390.8 1.0 copy-start.7
  390.8 1.2 copy-start.9
  390.8 1.4 copy-start.10
  390.8 1.5 copy-start.18
  392.3 1.5 copy-start.20
  392.3 1.5 copy-start.22
  392.3 1.5 copy-start.23
  392.3 1.5 copy-start.26
  487.3 1.9 copy-start.2
  489.2 1.9 copy-start.27
  491.7 1.0 copy-start.29
  491.7 1.7 copy-start.5
  491.8 1.7 copy-start.14
  491.8 1.7 copy-start.28
  493.5 1.0 copy-start.30
  493.5 1.0 copy-start.31
Sparse Core Ops, SparseCore 0:
  233.4 34.1 all-gather.12
  269.4 33.3 all-gather.18
  309.5 33.3 all-gather.20
  344.5 33.3 all-gather.14
  385.7 49.8 all-gather.22
  437.3 49.9 all-gather.16
where the time goes:
time: 569 us; the launch traced here: 563 us
  waiting for transfers between devices  224 us (39%)
  other arithmetic  173 us (30%)
  matrix products  95.8 us (17%)
  blocking collectives  28.1 us (5%)
  local copies, waits for them, and re-layouts  26.7 us (5%)
  between operations  13.9 us (2%)
    all_gather x6, waiting for transfers between devices, prefix_by_axis(): pieces = jax.tree.map(lambda part: lax.all_gather(part, axis), running)  223 us
    another operation x16, other arithmetic, block_parts(): jax.scipy.linalg.solve_triangular(system, right_side, lower=True, unit_di...  163 us
    all_to_all x1, blocking collectives, sum_at_owner(): tiles = lax.all_to_all(split_up(x, dim, devices), axis, 0, 0, tiled=True)  28.1 us
    dot_general x15, matrix products, chain_maps(): jnp.einsum('hij,hjv->hiv', later_map[0], earlier_map[1], precision=strict...  19.4 us
  transfers between devices with their start and end apart: 6, of which 6 were waited for; matrix products, arithmetic and copies ran while one was open for 2% of the time, Pallas kernels for 0%

commit v1 on v0

v1 whole, which is shorter than its diff:
```python
import functools

import jax
import jax.numpy as jnp
from jax import lax
from jax.experimental import pallas as pl
from jax.experimental.pallas import tpu as pltpu
from jax.sharding import Mesh
from jax.sharding import PartitionSpec as P

SEQ = ("seq_0", "seq_1", "seq_2")
SEQ_HEADS = ("seq_0", "seq_1", "seq_2", "heads")
F32 = jnp.float32
BF16 = jnp.bfloat16
HIGHEST = lax.Precision.HIGHEST
norm_eps = 1e-12
unit_eps = 1e-06

NN = (((1,), (0,)), ((), ()))
NT = (((1,), (1,)), ((), ()))
TN = (((0,), (0,)), ((), ()))


def dot(a, b, dims=NN):
    return lax.dot_general(a, b, dims, preferred_element_type=F32)


def split(x):
    high = x.astype(BF16)
    low = (x - high.astype(F32)).astype(BF16)
    return high, low


def dot_split(a, b, dims=NN):
    return dot(a[0], b[0], dims) + (dot(a[0], b[1], dims) + dot(a[1], b[0], dims))


def spread(parts):
    half = parts[0].shape[0]
    out = []
    for part in parts:
        zero = jnp.zeros((half, half), part.dtype)
        top = jnp.concatenate([part[:, :half], zero], axis=1)
        bottom = jnp.concatenate([zero, part[:, half:]], axis=1)
        out.append(jnp.concatenate([top, bottom], axis=0))
    return tuple(out)


def unit_lower_inverse(lower, row, col):
    size = lower.shape[0]
    half = size // 2
    compact = jnp.concatenate([lower[:half, :half], lower[half:, half:]], axis=1)
    r = row[:half, :]
    c = col[:half, :] % half
    base = 8
    diag = jnp.where(r // base == c // base, compact, 0.0)
    s1 = split(diag)
    d2 = dot_split(s1, spread(s1))
    s2 = split(d2)
    f2 = spread(s2)
    d3 = dot_split(s1, f2)
    d4 = dot_split(s2, f2)
    inv = jnp.where(r == c, 1.0, 0.0) - diag + d2 - d3
    inv = inv + dot_split(split(inv), spread(split(d4)))
    width = base
    while width < half:
        across = (r // (2 * width) == c // (2 * width)) & (r // width != c // width)
        off = split(jnp.where(across, compact, 0.0))
        si = split(inv)
        step = split(dot_split(si, spread(off)))
        inv = inv - dot_split(step, spread(si))
        width *= 2
    top, bottom = inv[:, :half], inv[:, half:]
    corner = split(dot_split(split(bottom), split(lower[half:, :half])))
    corner = -dot_split(corner, split(top))
    return jnp.concatenate(
        [
            jnp.concatenate([top, jnp.zeros((half, half), F32)], axis=1),
            jnp.concatenate([corner, bottom], axis=1),
        ],
        axis=0,
    )


def local_kernel(q_ref, k_ref, v_ref, w_ref, d_ref, maps_ref, own_ref, reach_ref, rows, cols):
    size, width = k_ref.shape
    group = maps_ref.shape[0]
    pair = pl.program_id(0)
    row = lax.broadcasted_iota(jnp.int32, (size, size), 0)
    col = lax.broadcasted_iota(jnp.int32, (size, size), 1)

    @pl.when(pair == 0)
    def _():
        tri = jnp.where(row >= col, 1.0, 0.0).astype(F32)
        eye = jnp.where(row == col, 1.0, 0.0).astype(F32)
        rate = d_ref[...]
        cols[...] = lax.dot_general(tri, rate, NN, precision=HIGHEST, preferred_element_type=F32)
        rows[0] = lax.dot_general(
            rate, tri, (((0,), (1,)), ((), ())), precision=HIGHEST, preferred_element_type=F32
        )
        rows[1] = lax.dot_general(
            w_ref[...], eye, TN, precision=HIGHEST, preferred_element_type=F32
        )

    q = q_ref[...]
    k = k_ref[...]
    kf = k.astype(F32)
    qf = q.astype(F32)
    k2 = kf * kf
    rk_col = lax.rsqrt(jnp.sum(k2, axis=1, keepdims=True) + unit_eps)
    rq_col = lax.rsqrt(jnp.sum(qf * qf, axis=1, keepdims=True) + unit_eps)
    ones = jnp.ones((8, width), F32)
    k2_row = lax.dot_general(ones, k2, NT, precision=HIGHEST, preferred_element_type=F32)
    rk_row = lax.rsqrt(k2_row[0:1, :] + unit_eps)
    key_dots = dot(k, k, NT) * rk_col * rk_row
    query_dots = dot(q, k, NT) * rq_col * rk_row
    unit_q = qf * rq_col
    heads = w_ref.shape[1]
    lane = lax.broadcasted_iota(jnp.int32, (size, heads), 1)
    eye_k = jnp.where(
        lax.broadcasted_iota(jnp.int32, (width, width), 0)
        == lax.broadcasted_iota(jnp.int32, (width, width), 1),
        1.0,
        0.0,
    )
    for member in range(group):
        head = pair * group + member
        g_col = -jnp.sum(jnp.where(lane == head, cols[...], 0.0), axis=1, keepdims=True)
        w_col = jnp.sum(jnp.where(lane == head, w_ref[...], 0.0), axis=1, keepdims=True)
        g_row = -rows[0, pl.ds(head, 1), :]
        w_row = rows[1, pl.ds(head, 1), :]
        ratios = jnp.exp(jnp.minimum(g_col - g_row, 0.0))
        lower = jnp.where(row > col, w_col * ratios * key_dots, 0.0)
        mixing = split(jnp.where(row >= col, ratios * query_dots, 0.0))
        inv = unit_lower_inverse(lower, row, col)
        g_end = g_row[:, size - 1 : size]
        gamma_col = jnp.exp(g_col)
        trail = jnp.exp(g_end - g_col) * rk_col
        on_keys = split(inv * (w_row * jnp.exp(g_row) * rk_row))
        on_values = split(inv * w_row)
        v = v_ref[:, member * width : (member + 1) * width]
        solved = jnp.concatenate(
            [
                dot(on_keys[0], k) + dot(on_keys[1], k),
                dot(on_values[0], v) + dot(on_values[1], v),
            ],
            axis=1,
        )
        mixed = dot_split(mixing, split(solved))
        tail = split(trail * solved)
        moved = dot(k, tail[0], TN) + dot(k, tail[1], TN)
        maps_ref[member, :, :width] = jnp.exp(g_end) * eye_k - moved[:, :width]
        maps_ref[member, :, width:] = moved[:, width:]
        reach_ref[member] = gamma_col * unit_q - mixed[:, :width]
        own_ref[member] = mixed[:, width:]


def local_work(queries, key_vecs, values, strength, decay_rate):
    size, pairs, width = queries.shape
    heads = values.shape[1]
    group = heads // pairs
    flat_q = queries.reshape(size, pairs * width)
    flat_k = key_vecs.reshape(size, pairs * width)
    flat_v = values.reshape(size, heads * width)
    one = pl.BlockSpec((size, width), lambda i: (0, i))
    small = pl.BlockSpec((size, heads), lambda i: (0, 0))
    return pl.pallas_call(
        local_kernel,
        grid=(pairs,),
        in_specs=[one, one, pl.BlockSpec((size, group * width), lambda i: (0, i)), small, small],
        out_specs=[
            pl.BlockSpec((group, width, 2 * width), lambda i: (i, 0, 0)),
            pl.BlockSpec((group, size, width), lambda i: (i, 0, 0)),
            pl.BlockSpec((group, size, width), lambda i: (i, 0, 0)),
        ],
        out_shape=[
            jax.ShapeDtypeStruct((heads, width, 2 * width), F32),
            jax.ShapeDtypeStruct((heads, size, width), F32),
            jax.ShapeDtypeStruct((heads, size, width), F32),
        ],
        scratch_shapes=[pltpu.VMEM((2, heads, size), F32), pltpu.VMEM((size, heads), F32)],
        compiler_params=pltpu.CompilerParams(dimension_semantics=("arbitrary",)),
        name="local_work",
    )(flat_q, flat_k, flat_v, strength, decay_rate)


def remote(src, dst, send, recv, target):
    return pltpu.make_async_remote_copy(
        src_ref=src,
        dst_ref=dst,
        send_sem=send,
        recv_sem=recv,
        device_id=target,
        device_id_type=pl.DeviceIdType.MESH,
    )


def prefix_kernel(
    maps_ref, out_ref, arrived, prefix, lower_map, plane, states, incoming, passing,
    send_maps, recv_maps, send_pair, recv_pair, send_chain, recv_chain, send_down, recv_down,
):
    width = maps_ref.shape[1]
    z = lax.axis_index("seq_0")
    x = lax.axis_index("seq_1")
    y = lax.axis_index("seq_2")
    upper = x // 2
    side = x % 2
    place = side * 4 + y
    mine = ((side + upper) % 2) * 4 + y
    mirror = 3 - x

    def peer(step):
        p = (place + step) % 8
        target = {"seq_1": upper * 2 + p // 4, "seq_2": p % 4}
        head = ((p // 4 + upper) % 2) * 4 + p % 4
        return p, target, head

    def beside(dz, at):
        return {"seq_0": (z + dz + 4) % 4, "seq_1": at}

    barrier = pltpu.get_barrier_semaphore()
    greeted = [peer(step)[1] for step in range(1, 8)]
    greeted += [{"seq_1": mirror}]
    greeted += [beside(dz, at) for dz in (1, -1) for at in (x, mirror)]
    for target in greeted:
        pl.semaphore_signal(barrier, inc=1, device_id=target, device_id_type=pl.DeviceIdType.MESH)
    pl.semaphore_wait(barrier, len(greeted))

    for step in range(1, 8):
        p, target, head = peer(step)
        remote(
            maps_ref.at[head], arrived.at[place], send_maps.at[step], recv_maps.at[place], target
        ).start()
    arrived[place] = maps_ref[mine]

    def wait_map(s):
        @pl.when(place != s)
        def _():
            remote(
                maps_ref.at[0], arrived.at[s], send_maps.at[0], recv_maps.at[s], {"seq_1": mirror}
            ).wait_recv()

    def then(later, running):
        moved = dot_split(split(later[:, :width]), split(running))
        return jnp.concatenate([moved[:, :width], moved[:, width:] + later[:, width:]], axis=1)

    wait_map(0)
    running = arrived[0]
    prefix[0] = running
    for s in range(1, 8):
        wait_map(s)
        running = then(arrived[s], running)
        prefix[s] = running

    pair = remote(prefix.at[7], lower_map, send_pair, recv_pair, {"seq_1": mirror})

    @pl.when(upper == 0)
    def _():
        pair.start()

    @pl.when(upper == 1)
    def _():
        pair.wait_recv()
        plane[...] = then(prefix[7], lower_map[...])

    chain = [
        remote(passing, incoming, send_chain.at[i], recv_chain, beside(1, at))
        for i, at in enumerate((x, mirror))
    ]

    @pl.when(z == 0)
    def _():
        incoming[...] = jnp.zeros_like(incoming)

    @pl.when(z > 0)
    def _():
        chain[0].wait_recv()

    before = split(incoming[...])

    @pl.when((upper == 1) & (z < 3))
    def _():
        passing[...] = dot_split(split(plane[:, :width]), before) + plane[:, width:]
        for copy in chain:
            copy.start()

    @pl.when(upper == 0)
    def _():
        states[0] = incoming[...]

    @pl.when(upper == 1)
    def _():
        states[0] = dot_split(split(lower_map[:, :width]), before) + lower_map[:, width:]

    ahead = split(states[0])
    for s in range(1, 8):
        states[s] = dot_split(split(prefix[s - 1, :, :width]), ahead) + prefix[s - 1, :, width:]

    for step in range(1, 8):
        p, target, head = peer(step)
        remote(
            states.at[p], out_ref.at[mine], send_down.at[step], recv_down.at[mine], target
        ).start()
    out_ref[mine] = states[place]
    for s in range(8):
        @pl.when(mine != s)
        def _():
            remote(
                states.at[0], out_ref.at[s], send_down.at[0], recv_down.at[s], {"seq_1": mirror}
            ).wait_recv()

    for step in range(1, 8):
        p, target, head = peer(step)
        remote(
            maps_ref.at[head], arrived.at[place], send_maps.at[step], recv_maps.at[place], target
        ).wait_send()
        remote(
            states.at[p], out_ref.at[mine], send_down.at[step], recv_down.at[mine], target
        ).wait_send()

    @pl.when(upper == 0)
    def _():
        pair.wait_send()

    @pl.when((upper == 1) & (z < 3))
    def _():
        for copy in chain:
            copy.wait_send()


def prefix_states(maps):
    heads, width, _ = maps.shape
    dma = pltpu.SemaphoreType.DMA
    vmem = pl.BlockSpec(memory_space=pltpu.VMEM)
    return pl.pallas_call(
        prefix_kernel,
        out_shape=jax.ShapeDtypeStruct((heads, width, width), F32),
        in_specs=[vmem],
        out_specs=vmem,
        scratch_shapes=[
            pltpu.VMEM((8, width, 2 * width), F32),
            pltpu.VMEM((8, width, 2 * width), F32),
            pltpu.VMEM((width, 2 * width), F32),
            pltpu.VMEM((width, 2 * width), F32),
            pltpu.VMEM((8, width, width), F32),
            pltpu.VMEM((width, width), F32),
            pltpu.VMEM((width, width), F32),
            dma((8,)),
            dma((8,)),
            dma,
            dma,
            dma((2,)),
            dma,
            dma((8,)),
            dma((8,)),
        ],
        compiler_params=pltpu.CompilerParams(collective_id=0, has_side_effects=True),
        name="prefix_states",
    )(maps)


def output_kernel(
    own_ref, reach_ref, state_ref, gain_ref, weight_hbm, out_ref,
    weight, flat, to_core, from_core, to_chip, from_chip, local,
    load_sem, send_core, recv_core, send_chip, recv_chip,
):
    heads, size, width = own_ref.shape
    rows = size // 4
    chunks, _, span = to_chip.shape
    me = lax.axis_index("heads")
    chip = me // 2
    core = me % 2
    other_core = {"heads": chip * 2 + 1 - core}
    other_chip = {"heads": (1 - chip) * 2 + core}

    load = pltpu.make_async_copy(weight_hbm, weight, load_sem)
    load.start()
    barrier = pltpu.get_barrier_semaphore()
    for target in (other_core, other_chip):
        pl.semaphore_signal(barrier, inc=1, device_id=target, device_id_type=pl.DeviceIdType.MESH)
    pl.semaphore_wait(barrier, 2)

    for head in range(heads):
        value = own_ref[head] + dot_split(split(reach_ref[head]), split(state_ref[head]))
        mean = jnp.mean(value * value, axis=1, keepdims=True)
        normed = value * lax.rsqrt(mean + norm_eps) * gain_ref[...]
        flat[:, head * width : (head + 1) * width] = normed.astype(BF16)
    load.wait()

    def rows_of(owner):
        return pl.ds(pl.multiple_of(owner * rows, rows), rows)

    def core_copy(c):
        return remote(
            to_core.at[c], from_core.at[c], send_core.at[c], recv_core.at[c], other_core
        )

    def chip_copy(c):
        return remote(
            to_chip.at[c], from_chip.at[c], send_chip.at[c], recv_chip.at[c], other_chip
        )

    far_mine = flat[rows_of((1 - chip) * 2 + core), :]
    far_theirs = flat[rows_of((1 - chip) * 2 + 1 - core), :]
    near_mine = flat[rows_of(me), :]
    near_theirs = flat[rows_of(chip * 2 + 1 - core), :]
    far = jnp.concatenate([far_theirs, far_mine], axis=0)
    near = jnp.concatenate([near_theirs, near_mine], axis=0)

    for c in range(chunks):
        part = dot(far, weight[:, c * span : (c + 1) * span])
        to_core[c] = part[:rows]
        core_copy(c).start()
        to_chip[c] = part[rows:]
    for c in range(chunks):
        core_copy(c).wait_recv()
        to_chip[c] = to_chip[c] + from_core[c]
        chip_copy(c).start()
    for c in range(chunks):
        part = dot(near, weight[:, c * span : (c + 1) * span])
        to_core[chunks + c] = part[:rows]
        core_copy(chunks + c).start()
        local[c] = part[rows:]
    for c in range(chunks):
        core_copy(chunks + c).wait_recv()
        local[c] = local[c] + from_core[chunks + c]
    for c in range(chunks):
        chip_copy(c).wait_recv()
        total = local[c] + from_chip[c]
        out_ref[:, c * span : (c + 1) * span] = total.astype(BF16)
    for c in range(chunks):
        core_copy(c).wait_send()
        core_copy(chunks + c).wait_send()
        chip_copy(c).wait_send()


def outputs(own, reach, states, norm_gain, w_out):
    heads, size, width = own.shape
    depth, model = w_out.shape
    chunks = 4
    span = model // chunks
    rows = size // 4
    dma = pltpu.SemaphoreType.DMA
    vmem = pl.BlockSpec(memory_space=pltpu.VMEM)
    return pl.pallas_call(
        output_kernel,
        out_shape=jax.ShapeDtypeStruct((rows, model), BF16),
        in_specs=[vmem, vmem, vmem, vmem, pl.BlockSpec(memory_space=pl.ANY)],
        out_specs=vmem,
        scratch_shapes=[
            pltpu.VMEM((depth, model), BF16),
            pltpu.VMEM((size, depth), BF16),
            pltpu.VMEM((2 * chunks, rows, span), F32),
            pltpu.VMEM((2 * chunks, rows, span), F32),
            pltpu.VMEM((chunks, rows, span), F32),
            pltpu.VMEM((chunks, rows, span), F32),
            pltpu.VMEM((chunks, rows, span), F32),
            dma,
            dma((2 * chunks,)),
            dma((2 * chunks,)),
            dma((chunks,)),
            dma((chunks,)),
        ],
        compiler_params=pltpu.CompilerParams(collective_id=1, has_side_effects=True),
        name="outputs",
    )(own, reach, states, norm_gain.reshape(1, width), w_out)


def body(queries, key_vecs, values, strength, decay_rate, norm_gain, w_out):
    maps, own, reach = local_work(queries, key_vecs, values, strength, decay_rate)
    states = prefix_states(maps)
    return outputs(own, reach, states, norm_gain, w_out)


def solution(mesh):
    finer = Mesh(
        mesh.devices.reshape(4, 4, 4, mesh.shape["heads"]), ("seq_0", "seq_1", "seq_2", "heads")
    )
    placed = (
        P(SEQ, "heads", None),
        P(SEQ, "heads", None),
        P(SEQ, "heads", None),
        P(SEQ, "heads"),
        P(SEQ, "heads"),
        P(),
        P("heads", None),
    )
    return jax.shard_map(
        body, mesh=finer, in_specs=placed, out_specs=P(SEQ_HEADS, None), check_vma=False
    )
```

time: 569 us -> 112 us (0.20)
  waiting for transfers between devices: 224 us -> 0 us
  other arithmetic: 173 us -> 0 us
  Pallas kernels: 0 us -> 102 us
  matrix products: 95.8 us -> 0 us
  blocking collectives: 28.1 us -> 0 us
  local copies, waits for them, and re-layouts: 26.7 us -> 8.41 us
  between operations: 13.9 us -> 0.02 us
    all_gather x6 -> x0, waiting for transfers between devices: 223 us -> none  [prefix_by_axis(): pieces = jax.tree.map(lambda part: lax.all_gather(part, axis), running)]
    another operation x26 -> x0, other arithmetic: 164 us -> none  [the longest x16 163 us: block_parts(): jax.scipy.linalg.solve_triangular(system, right_side, lower=True, unit_di...]
    pallas_call x0 -> x3, Pallas kernels: none -> 102 us  [the longest x1 48.5 us: prefix_states(): pl.pallas_call(prefix_kernel, out_shape=jax.ShapeDtypeStruct((heads, widt...]
    dot_general x66 -> x0, matrix products: 89.5 us -> none  [the longest x15 19.4 us: chain_maps(): jnp.einsum('hij,hjv->hiv', later_map[0], earlier_map[1], precision=strict...]
    all_to_all x1 -> x0, blocking collectives: 28.1 us -> none  [sum_at_owner(): tiles = lax.all_to_all(split_up(x, dim, devices), axis, 0, 0, tiled=True)]
    dynamic_slice x28 -> x0, local copies, waits for them, and re-layouts: 11 us -> none  [the longest x20 10.7 us: body(): lax.scan(analyse, jnp.zeros((), jnp.float32), blocks)]
    another operation x4 -> x0, matrix products: 6.37 us -> none  [block_parts(): jax.scipy.linalg.solve_triangular(system, right_side, lower=True, unit_di...]
  transfers between devices with their start and end apart: 6 -> 0, of which waited for: 6 -> 0; matrix products, arithmetic and copies ran while one was open for 2% -> 0% of each run, Pallas kernels for 0% -> 0%
where the time goes in v1:
time: 112 us; the launch traced here: 111 us
  Pallas kernels  102 us (91%)
  local copies, waits for them, and re-layouts  8.41 us (8%)
    pallas_call x1, Pallas kernels, prefix_states(): pl.pallas_call(prefix_kernel, out_shape=jax.ShapeDtypeStruct((heads, widt...  48.5 us
    pallas_call x1, Pallas kernels, local_work(): pl.pallas_call(local_kernel, grid=(pairs,), in_specs=[one, one, pl.BlockS...  29.1 us
    pallas_call x1, Pallas kernels, outputs(): pl.pallas_call(output_kernel, out_shape=jax.ShapeDtypeStruct((rows, model...  24.6 us
    unnamed x4, local copies, waits for them, and re-layouts  6.54 us

profile of v1, /device:TPU:192, one launch (start us, length us, event | category | flops | bytes accessed | tf_op | source)
XLA Modules:
  0.0 110.6 jit_solution(10729087997788234838)
XLA Ops:
  0.0 1.5 %copy.8.w_ref = f32[256,8]{1,0:T(8,128)} copy(f32[256,8]{0,1:T(8,128)} %param.10) | data formatting | bytes 16384 | tf_op args[3]
  1.5 1.5 %copy.9.d_ref = f32[256,8]{1,0:T(8,128)} copy(f32[256,8]{0,1:T(8,128)} %param.11) | data formatting | bytes 16384 | tf_op args[4]
  2.9 1.9 %copy.16 = bf16[32,8,8,128]{3,1,2,0:T(8,128)(2,1)} copy(bf16[32,8,8,128]{3,2,1,0:T(8,128)(2,1)} %bitcast.12) | data formatting | bytes 1048576
  4.9 1.9 %copy_bitcast_fusion.1 = (bf16[256,512]{1,0:T(8,128)(2,1)}, bf16[256,512]{1,0:T(8,128)(2,1)}) fusion(bf16[32,8,4,128]{3,2,1,0:T(4,128)(2,1)} %bitcast.13, bf16[32,8,4,128]{3,2,1,0:T(4,128)(2,1)} %bitcast.14), kind=kLoop, calls=%fused_computation.1 | loop fusion | bytes 1048576 | tf_op jit(solution)/shard_map/reshape | solution.py:163
  6.7 29.1 %local_work.1 = (f32[8,128,256]{2,1,0:T(8,128)}, f32[8,256,128]{2,1,0:T(8,128)}, f32[8,256,128]{2,1,0:T(8,128)}) custom-call(bf16[256,512]{1,0:T(8,128)(2,1)} %get-tuple-element.12.q_ref, bf16[256,512]{1,0:T(8,128)(2,1)} %get-tuple-element.11.k_ref, bf16[256,1024]{1,0:T(8,128)(2,1)} %bitcast.11, f32[256,8]{1,0:T(8,128)} %copy.8.w_ref, f32[256,8]{1,0:T(8,128)} %copy.9.d_ref), custom_call_target="tpu_custom_call" | custom-call | tf_op jit(solution)/shard_map/local_work/pallas_call | solution.py:167
  35.9 48.5 %prefix_states.1.state_ref = f32[8,128,128]{2,1,0:T(8,128)} custom-call(f32[8,128,256]{2,1,0:T(8,128)} %get-tuple-element.10.maps_ref), custom_call_target="tpu_custom_call" | custom-call | tf_op jit(solution)/shard_map/prefix_states/pallas_call | solution.py:335
  84.4 24.6 %outputs.1 = bf16[64,2048]{1,0:T(8,128)(2,1)} custom-call(f32[8,256,128]{2,1,0:T(8,128)} %get-tuple-element.8.own_ref, f32[8,256,128]{2,1,0:T(8,128)} %get-tuple-element.9.reach_ref, f32[8,128,128]{2,1,0:T(8,128)} %prefix_states.1.state_ref, f32[1,128]{1,0:T(1,128)} %bitcast.15, bf16[1024,2048]{1,0:T(8,128)(2,1)} %weight_hbm.1), custom_call_target="tpu_custom_call" | custom-call | tf_op jit(solution)/shard_map/outputs/pallas_call | solution.py:445
  108.9 1.7 %copy.18 = bf16[64,2048]{1,0:T(8,128)(2,1)} copy(bf16[64,2048]{1,0:T(8,128)(2,1)} %outputs.1) | data formatting | bytes 524288

commit v2 on v1

--- a/solution.py
+++ b/solution.py
@@ -35,15 +35,12 @@
     return dot(a[0], b[0], dims) + (dot(a[0], b[1], dims) + dot(a[1], b[0], dims))
 
 
-def spread(parts):
-    half = parts[0].shape[0]
-    out = []
-    for part in parts:
-        zero = jnp.zeros((half, half), part.dtype)
-        top = jnp.concatenate([part[:, :half], zero], axis=1)
-        bottom = jnp.concatenate([zero, part[:, half:]], axis=1)
-        out.append(jnp.concatenate([top, bottom], axis=0))
-    return tuple(out)
+def spread(part):
+    half = part.shape[0]
+    zero = jnp.zeros((half, half), part.dtype)
+    top = jnp.concatenate([part[:, :half], zero], axis=1)
+    bottom = jnp.concatenate([zero, part[:, half:]], axis=1)
+    return jnp.concatenate([top, bottom], axis=0)
 
 
 def unit_lower_inverse(lower, row, col):
@@ -54,134 +51,129 @@
     c = col[:half, :] % half
     base = 8
     diag = jnp.where(r // base == c // base, compact, 0.0)
-    s1 = split(diag)
-    d2 = dot_split(s1, spread(s1))
-    s2 = split(d2)
+    s1 = diag.astype(BF16)
+    d2 = dot(s1, spread(s1))
+    s2 = d2.astype(BF16)
     f2 = spread(s2)
-    d3 = dot_split(s1, f2)
-    d4 = dot_split(s2, f2)
+    d3 = dot(s1, f2)
+    d4 = dot(s2, f2)
     inv = jnp.where(r == c, 1.0, 0.0) - diag + d2 - d3
-    inv = inv + dot_split(split(inv), spread(split(d4)))
+    inv = inv + dot(inv.astype(BF16), spread(d4.astype(BF16)))
     width = base
     while width < half:
         across = (r // (2 * width) == c // (2 * width)) & (r // width != c // width)
-        off = split(jnp.where(across, compact, 0.0))
-        si = split(inv)
-        step = split(dot_split(si, spread(off)))
-        inv = inv - dot_split(step, spread(si))
+        off = jnp.where(across, compact, 0.0).astype(BF16)
+        si = inv.astype(BF16)
+        step = dot(si, spread(off)).astype(BF16)
+        inv = inv - dot(step, spread(si))
         width *= 2
-    top, bottom = inv[:, :half], inv[:, half:]
-    corner = split(dot_split(split(bottom), split(lower[half:, :half])))
-    corner = -dot_split(corner, split(top))
-    return jnp.concatenate(
+    si = inv.astype(BF16)
+    top, bottom = si[:, :half], si[:, half:]
+    high, low = split(lower)
+    corner = dot(bottom, high[half:, :half]).astype(BF16)
+    corner = -dot(corner, top)
+    rough = jnp.concatenate(
         [
-            jnp.concatenate([top, jnp.zeros((half, half), F32)], axis=1),
-            jnp.concatenate([corner, bottom], axis=1),
+            jnp.concatenate([top, jnp.zeros((half, half), BF16)], axis=1),
+            jnp.concatenate([corner.astype(BF16), bottom], axis=1),
         ],
         axis=0,
     )
-
-
-def local_kernel(q_ref, k_ref, v_ref, w_ref, d_ref, maps_ref, own_ref, reach_ref, rows, cols):
-    size, width = k_ref.shape
-    group = maps_ref.shape[0]
-    pair = pl.program_id(0)
+    eye = jnp.where(row == col, 1.0, 0.0)
+    known = rough.astype(F32)
+    residual = (eye - known) - (dot(high, rough) + dot(low, rough))
+    short = residual.astype(BF16)
+    series = (residual + dot(short, short)).astype(BF16)
+    return known + dot(rough, series)
+
+
+def column(table, head):
+    lane = lax.broadcasted_iota(jnp.int32, table.shape, 1)
+    return jnp.sum(jnp.where(lane == head, table, 0.0), axis=1, keepdims=True)
+
+
+def unpack_inputs(q_ref, k_ref, v_ref, w_ref, d_ref, q32, k32, v32, rows, cols):
+    q32[...] = q_ref[...].astype(F32)
+    k32[...] = k_ref[...].astype(F32)
+    v32[...] = v_ref[...].astype(F32)
+    size = d_ref.shape[1]
     row = lax.broadcasted_iota(jnp.int32, (size, size), 0)
     col = lax.broadcasted_iota(jnp.int32, (size, size), 1)
-
-    @pl.when(pair == 0)
-    def _():
-        tri = jnp.where(row >= col, 1.0, 0.0).astype(F32)
-        eye = jnp.where(row == col, 1.0, 0.0).astype(F32)
-        rate = d_ref[...]
-        cols[...] = lax.dot_general(tri, rate, NN, precision=HIGHEST, preferred_element_type=F32)
-        rows[0] = lax.dot_general(
-            rate, tri, (((0,), (1,)), ((), ())), precision=HIGHEST, preferred_element_type=F32
-        )
-        rows[1] = lax.dot_general(
-            w_ref[...], eye, TN, precision=HIGHEST, preferred_element_type=F32
-        )
-
-    q = q_ref[...]
-    k = k_ref[...]
-    kf = k.astype(F32)
-    qf = q.astype(F32)
+    tri = jnp.where(row >= col, 1.0, 0.0).astype(F32)
+    summed = lax.dot_general(d_ref[...], tri, NT, precision=HIGHEST, preferred_element_type=F32)
+    rows[0] = -summed
+    rows[1] = w_ref[...]
+    cols[0] = rows[0].T
+    cols[1] = rows[1].T
+
+
+def key_parts(k32, pair, pairs, size):
+    kf = k32[pl.ds(pair, size, stride=pairs), :]
     k2 = kf * kf
     rk_col = lax.rsqrt(jnp.sum(k2, axis=1, keepdims=True) + unit_eps)
-    rq_col = lax.rsqrt(jnp.sum(qf * qf, axis=1, keepdims=True) + unit_eps)
-    ones = jnp.ones((8, width), F32)
-    k2_row = lax.dot_general(ones, k2, NT, precision=HIGHEST, preferred_element_type=F32)
-    rk_row = lax.rsqrt(k2_row[0:1, :] + unit_eps)
+    ones = jnp.ones((8, kf.shape[1]), BF16)
+    high, low = split(k2)
+    total = dot(ones, high, NT) + dot(ones, low, NT)
+    rk_row = lax.rsqrt(total[0:1, :] + unit_eps)
+    return kf, kf.astype(BF16), rk_col, rk_row
+
+
+def decay_ratios(rows, cols, head):
+    g_row = rows[0, pl.ds(head, 1), :]
+    g_col = column(cols[0], head)
+    return g_row, g_col, jnp.exp(jnp.minimum(g_col - g_row, 0.0))
+
+
+def pair_maps(pair, k32, v32, rows, cols, maps_ref, solved_ref):
+    heads, width, _ = maps_ref.shape
+    size = rows.shape[2]
+    pairs = k32.shape[0] // size
+    group = heads // pairs
+    row = lax.broadcasted_iota(jnp.int32, (size, size), 0)
+    col = lax.broadcasted_iota(jnp.int32, (size, size), 1)
+    eye_k = jnp.where(row[:width, :width] == col[:width, :width], 1.0, 0.0)
+    kf, k, rk_col, rk_row = key_parts(k32, pair, pairs, size)
+    k_t = kf.T.astype(BF16)
     key_dots = dot(k, k, NT) * rk_col * rk_row
-    query_dots = dot(q, k, NT) * rq_col * rk_row
-    unit_q = qf * rq_col
-    heads = w_ref.shape[1]
-    lane = lax.broadcasted_iota(jnp.int32, (size, heads), 1)
-    eye_k = jnp.where(
-        lax.broadcasted_iota(jnp.int32, (width, width), 0)
-        == lax.broadcasted_iota(jnp.int32, (width, width), 1),
-        1.0,
-        0.0,
-    )
     for member in range(group):
         head = pair * group + member
-        g_col = -jnp.sum(jnp.where(lane == head, cols[...], 0.0), axis=1, keepdims=True)
-        w_col = jnp.sum(jnp.where(lane == head, w_ref[...], 0.0), axis=1, keepdims=True)
-        g_row = -rows[0, pl.ds(head, 1), :]
+        g_row, g_col, ratios = decay_ratios(rows, cols, head)
         w_row = rows[1, pl.ds(head, 1), :]
-        ratios = jnp.exp(jnp.minimum(g_col - g_row, 0.0))
+        w_col = column(cols[1], head)
         lower = jnp.where(row > col, w_col * ratios * key_dots, 0.0)
+        inv = split(unit_lower_inverse(lower, row, col) * w_row)
+        g_end = g_row[:, size - 1 : size]
+        keys = split(kf * (jnp.exp(g_col) * rk_col))
+        v = v32[pl.ds(head, size, stride=heads), :].astype(BF16)
+        right = jnp.concatenate([keys[0], v], axis=1)
+        both = dot(inv[0], right) + dot(inv[1], right)
+        on_keys = both[:, :width] + dot(inv[0], keys[1])
+        solved = jnp.concatenate([on_keys, both[:, width:]], axis=1)
+        solved_ref[head] = solved
+        tail = split((jnp.exp(g_end - g_col) * rk_col) * solved)
+        moved = dot(k_t, tail[0]) + dot(k_t, tail[1])
+        maps_ref[head, :, :width] = jnp.exp(g_end) * eye_k - moved[:, :width]
+        maps_ref[head, :, width:] = moved[:, width:]
+
+
+def pair_outputs(pair, q32, k32, rows, cols, solved_ref, own_ref, reach_ref):
+    heads, size, width = own_ref.shape
+    pairs = k32.shape[0] // size
+    group = heads // pairs
+    row = lax.broadcasted_iota(jnp.int32, (size, size), 0)
+    col = lax.broadcasted_iota(jnp.int32, (size, size), 1)
+    kf, k, rk_col, rk_row = key_parts(k32, pair, pairs, size)
+    qf = q32[pl.ds(pair, size, stride=pairs), :]
+    rq_col = lax.rsqrt(jnp.sum(qf * qf, axis=1, keepdims=True) + unit_eps)
+    query_dots = dot(qf.astype(BF16), k, NT) * rq_col * rk_row
+    unit_q = qf * rq_col
+    for member in range(group):
+        head = pair * group + member
+        g_row, g_col, ratios = decay_ratios(rows, cols, head)
         mixing = split(jnp.where(row >= col, ratios * query_dots, 0.0))
-        inv = unit_lower_inverse(lower, row, col)
-        g_end = g_row[:, size - 1 : size]
-        gamma_col = jnp.exp(g_col)
-        trail = jnp.exp(g_end - g_col) * rk_col
-        on_keys = split(inv * (w_row * jnp.exp(g_row) * rk_row))
-        on_values = split(inv * w_row)
-        v = v_ref[:, member * width : (member + 1) * width]
-        solved = jnp.concatenate(
-            [
-                dot(on_keys[0], k) + dot(on_keys[1], k),
-                dot(on_values[0], v) + dot(on_values[1], v),
-            ],
-            axis=1,
-        )
-        mixed = dot_split(mixing, split(solved))
-        tail = split(trail * solved)
-        moved = dot(k, tail[0], TN) + dot(k, tail[1], TN)
-        maps_ref[member, :, :width] = jnp.exp(g_end) * eye_k - moved[:, :width]
-        maps_ref[member, :, width:] = moved[:, width:]
-        reach_ref[member] = gamma_col * unit_q - mixed[:, :width]
-        own_ref[member] = mixed[:, width:]
-
-
-def local_work(queries, key_vecs, values, strength, decay_rate):
-    size, pairs, width = queries.shape
-    heads = values.shape[1]
-    group = heads // pairs
-    flat_q = queries.reshape(size, pairs * width)
-    flat_k = key_vecs.reshape(size, pairs * width)
-    flat_v = values.reshape(size, heads * width)
-    one = pl.BlockSpec((size, width), lambda i: (0, i))
-    small = pl.BlockSpec((size, heads), lambda i: (0, 0))
-    return pl.pallas_call(
-        local_kernel,
-        grid=(pairs,),
-        in_specs=[one, one, pl.BlockSpec((size, group * width), lambda i: (0, i)), small, small],
-        out_specs=[
-            pl.BlockSpec((group, width, 2 * width), lambda i: (i, 0, 0)),
-            pl.BlockSpec((group, size, width), lambda i: (i, 0, 0)),
-            pl.BlockSpec((group, size, width), lambda i: (i, 0, 0)),
-        ],
-        out_shape=[
-            jax.ShapeDtypeStruct((heads, width, 2 * width), F32),
-            jax.ShapeDtypeStruct((heads, size, width), F32),
-            jax.ShapeDtypeStruct((heads, size, width), F32),
-        ],
-        scratch_shapes=[pltpu.VMEM((2, heads, size), F32), pltpu.VMEM((size, heads), F32)],
-        compiler_params=pltpu.CompilerParams(dimension_semantics=("arbitrary",)),
-        name="local_work",
-    )(flat_q, flat_k, flat_v, strength, decay_rate)
+        mixed = dot_split(mixing, split(solved_ref[head]))
+        reach_ref[head] = jnp.exp(g_col) * unit_q - mixed[:, :width]
+        own_ref[head] = mixed[:, width:]
 
 
 def remote(src, dst, send, recv, target):
@@ -195,8 +187,10 @@
     )
 
 
-def prefix_kernel(
-    maps_ref, out_ref, arrived, prefix, lower_map, plane, states, incoming, passing,
+def front_kernel(
+    q_ref, k_ref, v_ref, w_ref, d_ref, own_ref, reach_ref, out_ref,
+    q32, k32, v32, rows, cols, maps_ref, solved_ref,
+    arrived, prefix, lower_map, plane, states, incoming, passing,
     send_maps, recv_maps, send_pair, recv_pair, send_chain, recv_chain, send_down, recv_down,
 ):
     width = maps_ref.shape[1]
@@ -224,14 +218,41 @@
     greeted += [beside(dz, at) for dz in (1, -1) for at in (x, mirror)]
     for target in greeted:
         pl.semaphore_signal(barrier, inc=1, device_id=target, device_id_type=pl.DeviceIdType.MESH)
-    pl.semaphore_wait(barrier, len(greeted))
-
-    for step in range(1, 8):
-        p, target, head = peer(step)
-        remote(
-            maps_ref.at[head], arrived.at[place], send_maps.at[step], recv_maps.at[place], target
-        ).start()
+
+    unpack_inputs(q_ref, k_ref, v_ref, w_ref, d_ref, q32, k32, v32, rows, cols)
+
+    def send_map(head):
+        p = ((head // 4 + upper) % 2) * 4 + head % 4
+        target = {"seq_1": upper * 2 + p // 4, "seq_2": p % 4}
+        return remote(
+            maps_ref.at[head], arrived.at[place], send_maps.at[head], recv_maps.at[place], target
+        )
+
+    def one_pair(step, carry):
+        pair = (mine // 2 + step) % 4
+        pair_maps(pair, k32, v32, rows, cols, maps_ref, solved_ref)
+
+        @pl.when(step == 1)
+        def _():
+            pl.semaphore_wait(barrier, len(greeted))
+
+        for member in range(2):
+            head = pair * 2 + member
+
+            @pl.when(head != mine)
+            def _():
+                send_map(head).start()
+
+        return carry
+
+    lax.fori_loop(1, 5, one_pair, 0)
     arrived[place] = maps_ref[mine]
+
+    def one_output(pair, carry):
+        pair_outputs(pair, q32, k32, rows, cols, solved_ref, own_ref, reach_ref)
+        return carry
+
+    lax.fori_loop(0, 4, one_output, 0)
 
     def wait_map(s):
         @pl.when(place != s)
@@ -311,9 +332,7 @@
 
     for step in range(1, 8):
         p, target, head = peer(step)
-        remote(
-            maps_ref.at[head], arrived.at[place], send_maps.at[step], recv_maps.at[place], target
-        ).wait_send()
+        send_map(head).wait_send()
         remote(
             states.at[p], out_ref.at[mine], send_down.at[step], recv_down.at[mine], target
         ).wait_send()
@@ -328,16 +347,28 @@
             copy.wait_send()
 
 
-def prefix_states(maps):
-    heads, width, _ = maps.shape
+def front(queries, key_vecs, values, strength, decay_rate):
+    size, pairs, width = queries.shape
+    heads = values.shape[1]
     dma = pltpu.SemaphoreType.DMA
     vmem = pl.BlockSpec(memory_space=pltpu.VMEM)
     return pl.pallas_call(
-        prefix_kernel,
-        out_shape=jax.ShapeDtypeStruct((heads, width, width), F32),
-        in_specs=[vmem],
-        out_specs=vmem,
+        front_kernel,
+        out_shape=[
+            jax.ShapeDtypeStruct((heads, size, width), F32),
+            jax.ShapeDtypeStruct((heads, size, width), F32),
+            jax.ShapeDtypeStruct((heads, width, width), F32),
+        ],
+        in_specs=[vmem] * 5,
+        out_specs=[vmem] * 3,
         scratch_shapes=[
+            pltpu.VMEM((size * pairs, width), F32),
+            pltpu.VMEM((size * pairs, width), F32),
+            pltpu.VMEM((size * heads, width), F32),
+            pltpu.VMEM((2, heads, size), F32),
+            pltpu.VMEM((2, size, heads), F32),
+            pltpu.VMEM((heads, width, 2 * width), F32),
+            pltpu.VMEM((heads, size, 2 * width), F32),
             pltpu.VMEM((8, width, 2 * width), F32),
             pltpu.VMEM((8, width, 2 * width), F32),
             pltpu.VMEM((width, 2 * width), F32),
@@ -355,8 +386,14 @@
             dma((8,)),
         ],
         compiler_params=pltpu.CompilerParams(collective_id=0, has_side_effects=True),
-        name="prefix_states",
-    )(maps)
+        name="front",
+    )(
+        queries.reshape(size * pairs, width),
+        key_vecs.reshape(size * pairs, width),
+        values.reshape(size * heads, width),
+        strength.T,
+        decay_rate.T,
+    )
 
 
 def output_kernel(
@@ -467,8 +504,7 @@
 
 
 def body(queries, key_vecs, values, strength, decay_rate, norm_gain, w_out):
-    maps, own, reach = local_work(queries, key_vecs, values, strength, decay_rate)
-    states = prefix_states(maps)
+    own, reach, states = front(queries, key_vecs, values, strength, decay_rate)
     return outputs(own, reach, states, norm_gain, w_out)
 
 

time: 112 us -> 84 us (0.75)
  Pallas kernels: 102 us -> 81.4 us
  local copies, waits for them, and re-layouts: 8.41 us -> 1.67 us
    pallas_call x2 -> x1, Pallas kernels: 77.6 us -> 56.8 us  [front(): pl.pallas_call(front_kernel, out_shape=[jax.ShapeDtypeStruct((heads, size...]
    unnamed x4 -> x1, local copies, waits for them, and re-layouts: 6.54 us -> 1.67 us
    reshape x1 -> x0, local copies, waits for them, and re-layouts: 1.87 us -> none  [local_work(): flat_k = key_vecs.reshape(size, pairs * width)]
where the time goes in v2:
time: 84 us; the launch traced here: 83 us
  Pallas kernels  81.4 us (97%)
  local copies, waits for them, and re-layouts  1.67 us (2%)
    pallas_call x1, Pallas kernels, front(): pl.pallas_call(front_kernel, out_shape=[jax.ShapeDtypeStruct((heads, size...  56.8 us
    pallas_call x1, Pallas kernels, outputs(): pl.pallas_call(output_kernel, out_shape=jax.ShapeDtypeStruct((rows, model...  24.6 us

profile of v2, /device:TPU:192, one launch (start us, length us, event | category | flops | bytes accessed | tf_op | source)
XLA Modules:
  0.0 83.0 jit_solution(8475142781341658061)
XLA Ops:
  0.0 56.8 %front.1 = (f32[8,256,128]{2,1,0:T(8,128)}, f32[8,256,128]{2,1,0:T(8,128)}, f32[8,128,128]{2,1,0:T(8,128)}) custom-call(bf16[1024,128]{1,0:T(8,128)(2,1)} %bitcast.7, bf16[1024,128]{1,0:T(8,128)(2,1)} %bitcast.8, bf16[2048,128]{1,0:T(8,128)(2,1)} %bitcast.6, f32[8,256]{1,0:T(8,128)} %bitcast.9, f32[8,256]{1,0:T(8,128)} %bitcast.10), custom_call_target="tpu_custom_call" | custom-call | tf_op jit(solution)/shard_map/front/pallas_call | solution.py:355
  56.8 24.6 %outputs.1 = bf16[64,2048]{1,0:T(8,128)(2,1)} custom-call(f32[8,256,128]{2,1,0:T(8,128)} %get-tuple-element.8.own_ref, f32[8,256,128]{2,1,0:T(8,128)} %get-tuple-element.9.reach_ref, f32[8,128,128]{2,1,0:T(8,128)} %get-tuple-element.10.state_ref, f32[1,128]{1,0:T(1,128)} %bitcast.11, bf16[1024,2048]{1,0:T(8,128)(2,1)} %weight_hbm.1), custom_call_target="tpu_custom_call" | custom-call | tf_op jit(solution)/shard_map/outputs/pallas_call | solution.py:482
  81.4 1.7 %copy.9 = bf16[64,2048]{1,0:T(8,128)(2,1)} copy(bf16[64,2048]{1,0:T(8,128)(2,1)} %outputs.1) | data formatting | bytes 524288

commit v3 on v2

--- a/solution.py
+++ b/solution.py
@@ -43,48 +43,52 @@
     return jnp.concatenate([top, bottom], axis=0)
 
 
-def unit_lower_inverse(lower, row, col):
-    size = lower.shape[0]
+def unit_lower_inverses(lowers, row, col):
+    size = row.shape[0]
     half = size // 2
-    compact = jnp.concatenate([lower[:half, :half], lower[half:, half:]], axis=1)
     r = row[:half, :]
     c = col[:half, :] % half
     base = 8
-    diag = jnp.where(r // base == c // base, compact, 0.0)
-    s1 = diag.astype(BF16)
-    d2 = dot(s1, spread(s1))
-    s2 = d2.astype(BF16)
-    f2 = spread(s2)
-    d3 = dot(s1, f2)
-    d4 = dot(s2, f2)
-    inv = jnp.where(r == c, 1.0, 0.0) - diag + d2 - d3
-    inv = inv + dot(inv.astype(BF16), spread(d4.astype(BF16)))
+    unit = jnp.where(r == c, 1.0, 0.0)
+    compact = [jnp.concatenate([x[:half, :half], x[half:, half:]], axis=1) for x in lowers]
+    diag = [jnp.where(r // base == c // base, x, 0.0) for x in compact]
+    s1 = [x.astype(BF16) for x in diag]
+    d2 = [dot(x, spread(x)) for x in s1]
+    s2 = [x.astype(BF16) for x in d2]
+    d3 = [dot(x, spread(y)) for x, y in zip(s1, s2)]
+    d4 = [dot(x, spread(x)).astype(BF16) for x in s2]
+    inv = [unit - x + y - z for x, y, z in zip(diag, d2, d3)]
+    inv = [x + dot(x.astype(BF16), spread(y)) for x, y in zip(inv, d4)]
     width = base
     while width < half:
         across = (r // (2 * width) == c // (2 * width)) & (r // width != c // width)
-        off = jnp.where(across, compact, 0.0).astype(BF16)
-        si = inv.astype(BF16)
-        step = dot(si, spread(off)).astype(BF16)
-        inv = inv - dot(step, spread(si))
+        off = [jnp.where(across, x, 0.0).astype(BF16) for x in compact]
+        si = [x.astype(BF16) for x in inv]
+        step = [dot(x, spread(y)).astype(BF16) for x, y in zip(si, off)]
+        inv = [x - dot(y, spread(z)) for x, y, z in zip(inv, step, si)]
         width *= 2
-    si = inv.astype(BF16)
-    top, bottom = si[:, :half], si[:, half:]
-    high, low = split(lower)
-    corner = dot(bottom, high[half:, :half]).astype(BF16)
-    corner = -dot(corner, top)
-    rough = jnp.concatenate(
-        [
-            jnp.concatenate([top, jnp.zeros((half, half), BF16)], axis=1),
-            jnp.concatenate([corner.astype(BF16), bottom], axis=1),
-        ],
-        axis=0,
-    )
+    si = [x.astype(BF16) for x in inv]
+    parts = [split(x) for x in lowers]
+    corner = [dot(x[:, half:], y[0][half:, :half]).astype(BF16) for x, y in zip(si, parts)]
+    corner = [(-dot(x, y[:, :half])).astype(BF16) for x, y in zip(corner, si)]
+    zero = jnp.zeros((half, half), BF16)
+    rough = [
+        jnp.concatenate(
+            [
+                jnp.concatenate([x[:, :half], zero], axis=1),
+                jnp.concatenate([y, x[:, half:]], axis=1),
+            ],
+            axis=0,
+        )
+        for x, y in zip(si, corner)
+    ]
     eye = jnp.where(row == col, 1.0, 0.0)
-    known = rough.astype(F32)
-    residual = (eye - known) - (dot(high, rough) + dot(low, rough))
-    short = residual.astype(BF16)
-    series = (residual + dot(short, short)).astype(BF16)
-    return known + dot(rough, series)
+    residual = [
+        (eye - x.astype(F32)) - (dot(y[0], x) + dot(y[1], x)) for x, y in zip(rough, parts)
+    ]
+    short = [x.astype(BF16) for x in residual]
+    series = [(x + dot(y, y)).astype(BF16) for x, y in zip(residual, short)]
+    return [x.astype(F32) + dot(x, y) for x, y in zip(rough, series)]
 
 
 def column(table, head):
@@ -124,7 +128,7 @@
     return g_row, g_col, jnp.exp(jnp.minimum(g_col - g_row, 0.0))
 
 
-def pair_maps(pair, k32, v32, rows, cols, maps_ref, solved_ref):
+def state_maps(chosen, k32, v32, rows, cols, maps_ref, solved_ref):
     heads, width, _ = maps_ref.shape
     size = rows.shape[2]
     pairs = k32.shape[0] // size
@@ -132,17 +136,19 @@
     row = lax.broadcasted_iota(jnp.int32, (size, size), 0)
     col = lax.broadcasted_iota(jnp.int32, (size, size), 1)
     eye_k = jnp.where(row[:width, :width] == col[:width, :width], 1.0, 0.0)
-    kf, k, rk_col, rk_row = key_parts(k32, pair, pairs, size)
-    k_t = kf.T.astype(BF16)
-    key_dots = dot(k, k, NT) * rk_col * rk_row
-    for member in range(group):
-        head = pair * group + member
-        g_row, g_col, ratios = decay_ratios(rows, cols, head)
-        w_row = rows[1, pl.ds(head, 1), :]
-        w_col = column(cols[1], head)
-        lower = jnp.where(row > col, w_col * ratios * key_dots, 0.0)
-        inv = split(unit_lower_inverse(lower, row, col) * w_row)
-        g_end = g_row[:, size - 1 : size]
+    keyed = [key_parts(k32, pair, pairs, size) for pair in chosen]
+    dots = [dot(k, k, NT) * rk_col * rk_row for _, k, rk_col, rk_row in keyed]
+    todo = [(pair * group + member, n) for n, pair in enumerate(chosen) for member in range(group)]
+    lowers = []
+    for head, n in todo:
+        _, _, ratios = decay_ratios(rows, cols, head)
+        lowers.append(jnp.where(row > col, column(cols[1], head) * ratios * dots[n], 0.0))
+    inverses = unit_lower_inverses(lowers, row, col)
+    scaled = [split(x * rows[1, pl.ds(head, 1), :]) for x, (head, _) in zip(inverses, todo)]
+    tails = []
+    for inv, (head, n) in zip(scaled, todo):
+        kf, _, rk_col, _ = keyed[n]
+        g_col = column(cols[0], head)
         keys = split(kf * (jnp.exp(g_col) * rk_col))
         v = v32[pl.ds(head, size, stride=heads), :].astype(BF16)
         right = jnp.concatenate([keys[0], v], axis=1)
@@ -150,8 +156,11 @@
         on_keys = both[:, :width] + dot(inv[0], keys[1])
         solved = jnp.concatenate([on_keys, both[:, width:]], axis=1)
         solved_ref[head] = solved
-        tail = split((jnp.exp(g_end - g_col) * rk_col) * solved)
-        moved = dot(k_t, tail[0]) + dot(k_t, tail[1])
+        g_end = rows[0, pl.ds(head, 1), :][:, size - 1 : size]
+        tails.append((g_end, split((jnp.exp(g_end - g_col) * rk_col) * solved)))
+    turned = [kf.T.astype(BF16) for kf, _, _, _ in keyed]
+    for (g_end, tail), (head, n) in zip(tails, todo):
+        moved = dot(turned[n], tail[0]) + dot(turned[n], tail[1])
         maps_ref[head, :, :width] = jnp.exp(g_end) * eye_k - moved[:, :width]
         maps_ref[head, :, width:] = moved[:, width:]
 
@@ -228,16 +237,16 @@
             maps_ref.at[head], arrived.at[place], send_maps.at[head], recv_maps.at[place], target
         )
 
-    def one_pair(step, carry):
-        pair = (mine // 2 + step) % 4
-        pair_maps(pair, k32, v32, rows, cols, maps_ref, solved_ref)
+    def some_heads(step, carry):
+        part = (mine // 4 + step) % 2
+        state_maps([part * 2, part * 2 + 1], k32, v32, rows, cols, maps_ref, solved_ref)
 
         @pl.when(step == 1)
         def _():
             pl.semaphore_wait(barrier, len(greeted))
 
-        for member in range(2):
-            head = pair * 2 + member
+        for member in range(4):
+            head = part * 4 + (mine + 1 + member) % 4
 
             @pl.when(head != mine)
             def _():
@@ -245,7 +254,7 @@
 
         return carry
 
-    lax.fori_loop(1, 5, one_pair, 0)
+    lax.fori_loop(1, 3, some_heads, 0)
     arrived[place] = maps_ref[mine]
 
     def one_output(pair, carry):
@@ -273,22 +282,47 @@
         running = then(arrived[s], running)
         prefix[s] = running
 
-    pair = remote(prefix.at[7], lower_map, send_pair, recv_pair, {"seq_1": mirror})
-
-    @pl.when(upper == 0)
-    def _():
-        pair.start()
-
-    @pl.when(upper == 1)
-    def _():
-        pair.wait_recv()
-        plane[...] = then(prefix[7], lower_map[...])
-
+    pair = [
+        remote(
+            prefix.at[7, :, pl.ds(part * width, width)],
+            lower_map.at[:, pl.ds(part * width, width)],
+            send_pair.at[part],
+            recv_pair.at[part],
+            {"seq_1": mirror},
+        )
+        for part in (1, 0)
+    ]
     chain = [
         remote(passing, incoming, send_chain.at[i], recv_chain, beside(1, at))
         for i, at in enumerate((x, mirror))
     ]
 
+    @pl.when(upper == 0)
+    def _():
+        for copy in pair:
+            copy.start()
+
+    @pl.when(upper == 1)
+    def _():
+        pair[0].wait_recv()
+
+    @pl.when((upper == 1) & (z == 0))
+    def _():
+        passing[...] = (
+            dot_split(split(prefix[7, :, :width]), split(lower_map[:, width:]))
+            + prefix[7, :, width:]
+        )
+        for copy in chain:
+            copy.start()
+
+    @pl.when(upper == 1)
+    def _():
+        pair[1].wait_recv()
+
+    @pl.when((upper == 1) & (z > 0))
+    def _():
+        plane[...] = then(prefix[7], lower_map[...])
+
     @pl.when(z == 0)
     def _():
         incoming[...] = jnp.zeros_like(incoming)
@@ -299,7 +333,7 @@
 
     before = split(incoming[...])
 
-    @pl.when((upper == 1) & (z < 3))
+    @pl.when((upper == 1) & (z > 0) & (z < 3))
     def _():
         passing[...] = dot_split(split(plane[:, :width]), before) + plane[:, width:]
         for copy in chain:
@@ -339,7 +373,8 @@
 
     @pl.when(upper == 0)
     def _():
-        pair.wait_send()
+        for copy in pair:
+            copy.wait_send()
 
     @pl.when((upper == 1) & (z < 3))
     def _():
@@ -378,8 +413,8 @@
             pltpu.VMEM((width, width), F32),
             dma((8,)),
             dma((8,)),
-            dma,
-            dma,
+            dma((2,)),
+            dma((2,)),
             dma((2,)),
             dma,
             dma((8,)),

time: 84 us -> 73.5 us (0.88)
  Pallas kernels: 81.4 us -> 71.6 us
    pallas_call x1, Pallas kernels: 56.8 us -> 50 us  [front(): pl.pallas_call(front_kernel, out_shape=[jax.ShapeDtypeStruct((heads, size...]
    pallas_call x1, Pallas kernels: 24.6 us -> 21.6 us  [outputs(): pl.pallas_call(output_kernel, out_shape=jax.ShapeDtypeStruct((rows, model...]
where the time goes in v3:
time: 73.5 us; the launch traced here: 73.2 us
  Pallas kernels  71.6 us (97%)
  local copies, waits for them, and re-layouts  1.67 us (2%)
    pallas_call x1, Pallas kernels, front(): pl.pallas_call(front_kernel, out_shape=[jax.ShapeDtypeStruct((heads, size...  50 us
    pallas_call x1, Pallas kernels, outputs(): pl.pallas_call(output_kernel, out_shape=jax.ShapeDtypeStruct((rows, model...  21.6 us
    unnamed x1, local copies, waits for them, and re-layouts  1.67 us

profile of v3, /device:TPU:192, one launch (start us, length us, event | category | flops | bytes accessed | tf_op | source)
XLA Modules:
  0.0 73.2 jit_solution(12531167130197888604)
XLA Ops:
  0.0 50.0 %front.1 = (f32[8,256,128]{2,1,0:T(8,128)}, f32[8,256,128]{2,1,0:T(8,128)}, f32[8,128,128]{2,1,0:T(8,128)}) custom-call(bf16[1024,128]{1,0:T(8,128)(2,1)} %bitcast.7, bf16[1024,128]{1,0:T(8,128)(2,1)} %bitcast.8, bf16[2048,128]{1,0:T(8,128)(2,1)} %bitcast.6, f32[8,256]{1,0:T(8,128)} %bitcast.9, f32[8,256]{1,0:T(8,128)} %bitcast.10), custom_call_target="tpu_custom_call" | custom-call | tf_op jit(solution)/shard_map/front/pallas_call | solution.py:390
  50.0 21.6 %outputs.1 = bf16[64,2048]{1,0:T(8,128)(2,1)} custom-call(f32[8,256,128]{2,1,0:T(8,128)} %get-tuple-element.8.own_ref, f32[8,256,128]{2,1,0:T(8,128)} %get-tuple-element.9.reach_ref, f32[8,128,128]{2,1,0:T(8,128)} %get-tuple-element.10.state_ref, f32[1,128]{1,0:T(1,128)} %bitcast.11, bf16[1024,2048]{1,0:T(8,128)(2,1)} %weight_hbm.1), custom_call_target="tpu_custom_call" | custom-call | tf_op jit(solution)/shard_map/outputs/pallas_call | solution.py:517
  71.6 1.7 %copy.9 = bf16[64,2048]{1,0:T(8,128)(2,1)} copy(bf16[64,2048]{1,0:T(8,128)(2,1)} %outputs.1) | data formatting | bytes 524288

commit v4 on v3

--- a/solution.py
+++ b/solution.py
@@ -1,5 +1,3 @@
-import functools
-
 import jax
 import jax.numpy as jnp
 from jax import lax
@@ -196,12 +194,16 @@
     )
 
 
-def front_kernel(
-    q_ref, k_ref, v_ref, w_ref, d_ref, own_ref, reach_ref, out_ref,
-    q32, k32, v32, rows, cols, maps_ref, solved_ref,
-    arrived, prefix, lower_map, plane, states, incoming, passing,
+def layer_kernel(
+    q_ref, k_ref, v_ref, w_ref, d_ref, gain_ref, weight_hbm, out_ref,
+    q32, k32, v32, rows, cols, maps_ref, solved_ref, own_ref, reach_ref,
+    arrived, prefix, lower_map, plane, states, incoming, passing, entering,
+    weight, flat, parts, from_core, to_chip, from_chip,
     send_maps, recv_maps, send_pair, recv_pair, send_chain, recv_chain, send_down, recv_down,
+    load_sem, send_core, recv_core, send_chip, recv_chip,
 ):
+    load = pltpu.make_async_copy(weight_hbm, weight, load_sem)
+    load.start()
     width = maps_ref.shape[1]
     z = lax.axis_index("seq_0")
     x = lax.axis_index("seq_1")
@@ -211,6 +213,11 @@
     place = side * 4 + y
     mine = ((side + upper) % 2) * 4 + y
     mirror = 3 - x
+    me = lax.axis_index("heads")
+    chip = me // 2
+    core = me % 2
+    other_core = {"heads": chip * 2 + 1 - core}
+    other_chip = {"heads": (1 - chip) * 2 + core}
 
     def peer(step):
         p = (place + step) % 8
@@ -225,6 +232,7 @@
     greeted = [peer(step)[1] for step in range(1, 8)]
     greeted += [{"seq_1": mirror}]
     greeted += [beside(dz, at) for dz in (1, -1) for at in (x, mirror)]
+    greeted += [other_core, other_chip]
     for target in greeted:
         pl.semaphore_signal(barrier, inc=1, device_id=target, device_id_type=pl.DeviceIdType.MESH)
 
@@ -351,25 +359,84 @@
     for s in range(1, 8):
         states[s] = dot_split(split(prefix[s - 1, :, :width]), ahead) + prefix[s - 1, :, width:]
 
+    def send_state(step):
+        p, target, head = peer(step)
+        return remote(
+            states.at[p], entering.at[mine], send_down.at[step], recv_down.at[mine], target
+        )
+
     for step in range(1, 8):
-        p, target, head = peer(step)
-        remote(
-            states.at[p], out_ref.at[mine], send_down.at[step], recv_down.at[mine], target
-        ).start()
-    out_ref[mine] = states[place]
-    for s in range(8):
-        @pl.when(mine != s)
+        send_state(step).start()
+    entering[mine] = states[place]
+    for head in range(8):
+        @pl.when(mine != head)
         def _():
             remote(
-                states.at[0], out_ref.at[s], send_down.at[0], recv_down.at[s], {"seq_1": mirror}
+                states.at[0],
+                entering.at[head],
+                send_down.at[0],
+                recv_down.at[head],
+                {"seq_1": mirror},
             ).wait_recv()
+
+    heads, size, _ = own_ref.shape
+    half = size // 2
+    quarter = size // 4
+    chunks, _, span = to_chip.shape
+
+    def emit(side):
+        here = pl.ds(pl.multiple_of(side * half, half), half)
+        entry = [split(entering[head]) for head in range(heads)]
+        value = [
+            own_ref[head, here, :] + dot_split(split(reach_ref[head, here, :]), entry[head])
+            for head in range(heads)
+        ]
+        mean = [jnp.mean(x * x, axis=1, keepdims=True) for x in value]
+        normed = [x * lax.rsqrt(m + norm_eps) * gain_ref[...] for x, m in zip(value, mean)]
+        for head in range(heads):
+            flat[:, head * width : (head + 1) * width] = normed[head].astype(BF16)
+
+    def core_copy(way, c):
+        return remote(
+            parts.at[way, c, 1 - core],
+            from_core.at[way, c],
+            send_core.at[way, c],
+            recv_core.at[way, c],
+            other_core,
+        )
+
+    def chip_copy(c):
+        return remote(
+            to_chip.at[c], from_chip.at[c], send_chip.at[c], recv_chip.at[c], other_chip
+        )
+
+    def project(way):
+        for c in range(chunks):
+            part = dot(flat[...], weight[:, c * span : (c + 1) * span])
+            parts[way, c, 0] = part[:quarter]
+            parts[way, c, 1] = part[quarter:]
+            core_copy(way, c).start()
+
+    emit(1 - chip)
+    load.wait()
+    project(0)
+    for c in range(chunks):
+        core_copy(0, c).wait_recv()
+        to_chip[c] = parts[0, c, core] + from_core[0, c]
+        chip_copy(c).start()
+    emit(chip)
+    project(1)
+    for c in range(chunks):
+        core_copy(1, c).wait_recv()
+    for c in range(chunks):
+        chip_copy(c).wait_recv()
+        total = parts[1, c, core] + from_core[1, c] + from_chip[c]
+        out_ref[:, c * span : (c + 1) * span] = total.astype(BF16)
 
     for step in range(1, 8):
         p, target, head = peer(step)
         send_map(head).wait_send()
-        remote(
-            states.at[p], out_ref.at[mine], send_down.at[step], recv_down.at[mine], target
-        ).wait_send()
+        send_state(step).wait_send()
 
     @pl.when(upper == 0)
     def _():
@@ -381,21 +448,26 @@
         for copy in chain:
             copy.wait_send()
 
-
-def front(queries, key_vecs, values, strength, decay_rate):
+    for c in range(chunks):
+        core_copy(0, c).wait_send()
+        core_copy(1, c).wait_send()
+        chip_copy(c).wait_send()
+
+
+def body(queries, key_vecs, values, strength, decay_rate, norm_gain, w_out):
     size, pairs, width = queries.shape
     heads = values.shape[1]
+    depth, model = w_out.shape
+    chunks = 8
+    span = model // chunks
+    quarter = size // 4
     dma = pltpu.SemaphoreType.DMA
     vmem = pl.BlockSpec(memory_space=pltpu.VMEM)
     return pl.pallas_call(
-        front_kernel,
-        out_shape=[
-            jax.ShapeDtypeStruct((heads, size, width), F32),
-            jax.ShapeDtypeStruct((heads, size, width), F32),
-            jax.ShapeDtypeStruct((heads, width, width), F32),
-        ],
-        in_specs=[vmem] * 5,
-        out_specs=[vmem] * 3,
+        layer_kernel,
+        out_shape=jax.ShapeDtypeStruct((quarter, model), BF16),
+        in_specs=[vmem] * 6 + [pl.BlockSpec(memory_space=pl.ANY)],
+        out_specs=vmem,
         scratch_shapes=[
             pltpu.VMEM((size * pairs, width), F32),
             pltpu.VMEM((size * pairs, width), F32),
@@ -404,6 +476,8 @@
             pltpu.VMEM((2, size, heads), F32),
             pltpu.VMEM((heads, width, 2 * width), F32),
             pltpu.VMEM((heads, size, 2 * width), F32),
+            pltpu.VMEM((heads, size, width), F32),
+            pltpu.VMEM((heads, size, width), F32),
             pltpu.VMEM((8, width, 2 * width), F32),
             pltpu.VMEM((8, width, 2 * width), F32),
             pltpu.VMEM((width, 2 * width), F32),
@@ -411,6 +485,13 @@
             pltpu.VMEM((8, width, width), F32),
             pltpu.VMEM((width, width), F32),
             pltpu.VMEM((width, width), F32),
+            pltpu.VMEM((heads, width, width), F32),
+            pltpu.VMEM((depth, model), BF16),
+            pltpu.VMEM((size // 2, depth), BF16),
+            pltpu.VMEM((2, chunks, 2, quarter, span), F32),
+            pltpu.VMEM((2, chunks, quarter, span), F32),
+            pltpu.VMEM((chunks, quarter, span), F32),
+            pltpu.VMEM((chunks, quarter, span), F32),
             dma((8,)),
             dma((8,)),
             dma((2,)),
@@ -419,128 +500,23 @@
             dma,
             dma((8,)),
             dma((8,)),
+            dma,
+            dma((2, chunks)),
+            dma((2, chunks)),
+            dma((chunks,)),
+            dma((chunks,)),
         ],
         compiler_params=pltpu.CompilerParams(collective_id=0, has_side_effects=True),
-        name="front",
+        name="layer",
     )(
         queries.reshape(size * pairs, width),
         key_vecs.reshape(size * pairs, width),
         values.reshape(size * heads, width),
         strength.T,
         decay_rate.T,
+        norm_gain.reshape(1, width),
+        w_out,
     )
-
-
-def output_kernel(
-    own_ref, reach_ref, state_ref, gain_ref, weight_hbm, out_ref,
-    weight, flat, to_core, from_core, to_chip, from_chip, local,
-    load_sem, send_core, recv_core, send_chip, recv_chip,
-):
-    heads, size, width = own_ref.shape
-    rows = size // 4
-    chunks, _, span = to_chip.shape
-    me = lax.axis_index("heads")
-    chip = me // 2
-    core = me % 2
-    other_core = {"heads": chip * 2 + 1 - core}
-    other_chip = {"heads": (1 - chip) * 2 + core}
-
-    load = pltpu.make_async_copy(weight_hbm, weight, load_sem)
-    load.start()
-    barrier = pltpu.get_barrier_semaphore()
-    for target in (other_core, other_chip):
-        pl.semaphore_signal(barrier, inc=1, device_id=target, device_id_type=pl.DeviceIdType.MESH)
-    pl.semaphore_wait(barrier, 2)
-
-    for head in range(heads):
-        value = own_ref[head] + dot_split(split(reach_ref[head]), split(state_ref[head]))
-        mean = jnp.mean(value * value, axis=1, keepdims=True)
-        normed = value * lax.rsqrt(mean + norm_eps) * gain_ref[...]
-        flat[:, head * width : (head + 1) * width] = normed.astype(BF16)
-    load.wait()
-
-    def rows_of(owner):
-        return pl.ds(pl.multiple_of(owner * rows, rows), rows)
-
-    def core_copy(c):
-        return remote(
-            to_core.at[c], from_core.at[c], send_core.at[c], recv_core.at[c], other_core
-        )
-
-    def chip_copy(c):
-        return remote(
-            to_chip.at[c], from_chip.at[c], send_chip.at[c], recv_chip.at[c], other_chip
-        )
-
-    far_mine = flat[rows_of((1 - chip) * 2 + core), :]
-    far_theirs = flat[rows_of((1 - chip) * 2 + 1 - core), :]
-    near_mine = flat[rows_of(me), :]
-    near_theirs = flat[rows_of(chip * 2 + 1 - core), :]
-    far = jnp.concatenate([far_theirs, far_mine], axis=0)
-    near = jnp.concatenate([near_theirs, near_mine], axis=0)
-
-    for c in range(chunks):
-        part = dot(far, weight[:, c * span : (c + 1) * span])
-        to_core[c] = part[:rows]
-        core_copy(c).start()
-        to_chip[c] = part[rows:]
-    for c in range(chunks):
-        core_copy(c).wait_recv()
-        to_chip[c] = to_chip[c] + from_core[c]
-        chip_copy(c).start()
-    for c in range(chunks):
-        part = dot(near, weight[:, c * span : (c + 1) * span])
-        to_core[chunks + c] = part[:rows]
-        core_copy(chunks + c).start()
-        local[c] = part[rows:]
-    for c in range(chunks):
-        core_copy(chunks + c).wait_recv()
-        local[c] = local[c] + from_core[chunks + c]
-    for c in range(chunks):
-        chip_copy(c).wait_recv()
-        total = local[c] + from_chip[c]
-        out_ref[:, c * span : (c + 1) * span] = total.astype(BF16)
-    for c in range(chunks):
-        core_copy(c).wait_send()
-        core_copy(chunks + c).wait_send()
-        chip_copy(c).wait_send()
-
-
-def outputs(own, reach, states, norm_gain, w_out):
-    heads, size, width = own.shape
-    depth, model = w_out.shape
-    chunks = 4
-    span = model // chunks
-    rows = size // 4
-    dma = pltpu.SemaphoreType.DMA
-    vmem = pl.BlockSpec(memory_space=pltpu.VMEM)
-    return pl.pallas_call(
-        output_kernel,
-        out_shape=jax.ShapeDtypeStruct((rows, model), BF16),
-        in_specs=[vmem, vmem, vmem, vmem, pl.BlockSpec(memory_space=pl.ANY)],
-        out_specs=vmem,
-        scratch_shapes=[
-            pltpu.VMEM((depth, model), BF16),
-            pltpu.VMEM((size, depth), BF16),
-            pltpu.VMEM((2 * chunks, rows, span), F32),
-            pltpu.VMEM((2 * chunks, rows, span), F32),
-            pltpu.VMEM((chunks, rows, span), F32),
-            pltpu.VMEM((chunks, rows, span), F32),
-            pltpu.VMEM((chunks, rows, span), F32),
-            dma,
-            dma((2 * chunks,)),
-            dma((2 * chunks,)),
-            dma((chunks,)),
-            dma((chunks,)),
-        ],
-        compiler_params=pltpu.CompilerParams(collective_id=1, has_side_effects=True),
-        name="outputs",
-    )(own, reach, states, norm_gain.reshape(1, width), w_out)
-
-
-def body(queries, key_vecs, values, strength, decay_rate, norm_gain, w_out):
-    own, reach, states = front(queries, key_vecs, values, strength, decay_rate)
-    return outputs(own, reach, states, norm_gain, w_out)
 
 
 def solution(mesh):

time: 73.5 us -> 68.5 us (0.932)
  Pallas kernels: 71.6 us -> 66.7 us
    pallas_call x2 -> x1, Pallas kernels: 71.6 us -> 66.7 us  [body(): pl.pallas_call(layer_kernel, out_shape=jax.ShapeDtypeStruct((quarter, mod...]
where the time goes in v4:
time: 68.5 us; the launch traced here: 68.4 us
  Pallas kernels  66.7 us (97%)
  local copies, waits for them, and re-layouts  1.67 us (2%)
    pallas_call x1, Pallas kernels, body(): pl.pallas_call(layer_kernel, out_shape=jax.ShapeDtypeStruct((quarter, mod...  66.7 us
    unnamed x1, local copies, waits for them, and re-layouts  1.67 us

profile of v4, /device:TPU:192, one launch (start us, length us, event | category | flops | bytes accessed | tf_op | source)
XLA Modules:
  0.0 68.4 jit_solution(15371685312584988608)
XLA Ops:
  0.0 66.7 %layer.1 = bf16[64,2048]{1,0:T(8,128)(2,1)} custom-call(bf16[1024,128]{1,0:T(8,128)(2,1)} %bitcast.7, bf16[1024,128]{1,0:T(8,128)(2,1)} %bitcast.8, bf16[2048,128]{1,0:T(8,128)(2,1)} %bitcast.6, f32[8,256]{1,0:T(8,128)} %bitcast.9, f32[8,256]{1,0:T(8,128)} %bitcast.10, f32[1,128]{1,0:T(1,128)} %bitcast.11, bf16[1024,2048]{1,0:T(8,128)(2,1)} %weight_hbm.1), custom_call_target="tpu_custom_call" | custom-call | tf_op jit(solution)/shard_map/layer/pallas_call | solution.py:466
  66.7 1.7 %copy.9 = bf16[64,2048]{1,0:T(8,128)(2,1)} copy(bf16[64,2048]{1,0:T(8,128)(2,1)} %layer.1) | data formatting | bytes 524288

commit v5 on v4

--- a/solution.py
+++ b/solution.py
@@ -10,7 +10,6 @@
 SEQ_HEADS = ("seq_0", "seq_1", "seq_2", "heads")
 F32 = jnp.float32
 BF16 = jnp.bfloat16
-HIGHEST = lax.Precision.HIGHEST
 norm_eps = 1e-12
 unit_eps = 1e-06
 
@@ -94,15 +93,19 @@
     return jnp.sum(jnp.where(lane == head, table, 0.0), axis=1, keepdims=True)
 
 
-def unpack_inputs(q_ref, k_ref, v_ref, w_ref, d_ref, q32, k32, v32, rows, cols):
-    q32[...] = q_ref[...].astype(F32)
+def unpack_inputs(k_ref, v_ref, w_ref, d_ref, k32, v32, rows, cols):
     k32[...] = k_ref[...].astype(F32)
     v32[...] = v_ref[...].astype(F32)
     size = d_ref.shape[1]
     row = lax.broadcasted_iota(jnp.int32, (size, size), 0)
     col = lax.broadcasted_iota(jnp.int32, (size, size), 1)
-    tri = jnp.where(row >= col, 1.0, 0.0).astype(F32)
-    summed = lax.dot_general(d_ref[...], tri, NT, precision=HIGHEST, preferred_element_type=F32)
+    tri = jnp.where(row <= col, 1.0, 0.0).astype(BF16)
+    rest = d_ref[...]
+    summed = jnp.zeros_like(rest)
+    for _ in range(3):
+        part = rest.astype(BF16)
+        summed = summed + dot(part, tri)
+        rest = rest - part.astype(F32)
     rows[0] = -summed
     rows[1] = w_ref[...]
     cols[0] = rows[0].T
@@ -197,10 +200,10 @@
 def layer_kernel(
     q_ref, k_ref, v_ref, w_ref, d_ref, gain_ref, weight_hbm, out_ref,
     q32, k32, v32, rows, cols, maps_ref, solved_ref, own_ref, reach_ref,
-    arrived, prefix, lower_map, plane, states, incoming, passing, entering,
-    weight, flat, parts, from_core, to_chip, from_chip,
-    send_maps, recv_maps, send_pair, recv_pair, send_chain, recv_chain, send_down, recv_down,
-    load_sem, send_core, recv_core, send_chip, recv_chip,
+    arrived, prefix, lower_map, plane, lent, states, incoming, passing, entering,
+    weight, flat, parts, from_core, to_chip, from_chip, result,
+    send_maps, recv_maps, send_pair, recv_pair, send_chain, recv_chain, send_lent, recv_lent, send_down, recv_down,
+    load_sem, send_core, recv_core, send_chip, recv_chip, store_sem,
 ):
     load = pltpu.make_async_copy(weight_hbm, weight, load_sem)
     load.start()
@@ -232,11 +235,11 @@
     greeted = [peer(step)[1] for step in range(1, 8)]
     greeted += [{"seq_1": mirror}]
     greeted += [beside(dz, at) for dz in (1, -1) for at in (x, mirror)]
-    greeted += [other_core, other_chip]
+    greeted += [beside(2, x), other_core, other_chip]
     for target in greeted:
         pl.semaphore_signal(barrier, inc=1, device_id=target, device_id_type=pl.DeviceIdType.MESH)
 
-    unpack_inputs(q_ref, k_ref, v_ref, w_ref, d_ref, q32, k32, v32, rows, cols)
+    unpack_inputs(k_ref, v_ref, w_ref, d_ref, k32, v32, rows, cols)
 
     def send_map(head):
         p = ((head // 4 + upper) % 2) * 4 + head % 4
@@ -264,6 +267,8 @@
 
     lax.fori_loop(1, 3, some_heads, 0)
     arrived[place] = maps_ref[mine]
+
+    q32[...] = q_ref[...].astype(F32)
 
     def one_output(pair, carry):
         pair_outputs(pair, q32, k32, rows, cols, solved_ref, own_ref, reach_ref)
@@ -282,13 +287,16 @@
         moved = dot_split(split(later[:, :width]), split(running))
         return jnp.concatenate([moved[:, :width], moved[:, width:] + later[:, width:]], axis=1)
 
-    wait_map(0)
-    running = arrived[0]
-    prefix[0] = running
-    for s in range(1, 8):
+    pairs_of = []
+    for s in range(0, 8, 2):
         wait_map(s)
-        running = then(arrived[s], running)
-        prefix[s] = running
+        wait_map(s + 1)
+        pairs_of.append(then(arrived[s + 1], arrived[s]))
+    low_half = then(pairs_of[1], pairs_of[0])
+    high_half = then(pairs_of[3], pairs_of[2])
+    prefix[7] = then(high_half, low_half)
+    prefix[1] = pairs_of[0]
+    prefix[3] = low_half
 
     pair = [
         remote(
@@ -301,14 +309,24 @@
         for part in (1, 0)
     ]
     chain = [
-        remote(passing, incoming, send_chain.at[i], recv_chain, beside(1, at))
-        for i, at in enumerate((x, mirror))
+        remote(passing, incoming, send_chain.at[i], recv_chain, beside(dz, at))
+        for i, (dz, at) in enumerate(((1, x), (2, x), (1, mirror)))
     ]
+    lend = remote(plane, lent, send_lent, recv_lent, beside(1, x))
 
     @pl.when(upper == 0)
     def _():
         for copy in pair:
             copy.start()
+
+    def rest_of_prefixes():
+        prefix[0] = arrived[0]
+        prefix[2] = then(arrived[2], prefix[1])
+        prefix[4] = then(arrived[4], prefix[3])
+        prefix[5] = then(arrived[5], prefix[4])
+        prefix[6] = then(arrived[6], prefix[5])
+
+    rest_of_prefixes()
 
     @pl.when(upper == 1)
     def _():
@@ -320,8 +338,8 @@
             dot_split(split(prefix[7, :, :width]), split(lower_map[:, width:]))
             + prefix[7, :, width:]
         )
-        for copy in chain:
-            copy.start()
+        chain[0].start()
+        chain[2].start()
 
     @pl.when(upper == 1)
     def _():
@@ -331,6 +349,10 @@
     def _():
         plane[...] = then(prefix[7], lower_map[...])
 
+    @pl.when((upper == 1) & (z == 2))
+    def _():
+        lend.start()
+
     @pl.when(z == 0)
     def _():
         incoming[...] = jnp.zeros_like(incoming)
@@ -339,13 +361,25 @@
     def _():
         chain[0].wait_recv()
 
+    @pl.when((upper == 1) & (z == 3))
+    def _():
+        lend.wait_recv()
+        incoming[...] = (
+            dot_split(split(lent[:, :width]), split(incoming[...])) + lent[:, width:]
+        )
+
     before = split(incoming[...])
 
     @pl.when((upper == 1) & (z > 0) & (z < 3))
     def _():
         passing[...] = dot_split(split(plane[:, :width]), before) + plane[:, width:]
-        for copy in chain:
-            copy.start()
+
+        @pl.when(z == 1)
+        def _():
+            chain[0].start()
+            chain[1].start()
+
+        chain[2].start()
 
     @pl.when(upper == 0)
     def _():
@@ -368,33 +402,19 @@
     for step in range(1, 8):
         send_state(step).start()
     entering[mine] = states[place]
-    for head in range(8):
-        @pl.when(mine != head)
-        def _():
-            remote(
-                states.at[0],
-                entering.at[head],
-                send_down.at[0],
-                recv_down.at[head],
-                {"seq_1": mirror},
-            ).wait_recv()
-
     heads, size, _ = own_ref.shape
     half = size // 2
     quarter = size // 4
     chunks, _, span = to_chip.shape
 
-    def emit(side):
+    def emit(side, head):
         here = pl.ds(pl.multiple_of(side * half, half), half)
-        entry = [split(entering[head]) for head in range(heads)]
-        value = [
-            own_ref[head, here, :] + dot_split(split(reach_ref[head, here, :]), entry[head])
-            for head in range(heads)
-        ]
-        mean = [jnp.mean(x * x, axis=1, keepdims=True) for x in value]
-        normed = [x * lax.rsqrt(m + norm_eps) * gain_ref[...] for x, m in zip(value, mean)]
-        for head in range(heads):
-            flat[:, head * width : (head + 1) * width] = normed[head].astype(BF16)
+        value = own_ref[head, here, :] + dot_split(
+            split(reach_ref[head, here, :]), split(entering[head])
+        )
+        mean = jnp.mean(value * value, axis=1, keepdims=True)
+        normed = value * lax.rsqrt(mean + norm_eps) * gain_ref[...]
+        flat[:, pl.ds(pl.multiple_of(head * width, width), width)] = normed.astype(BF16)
 
     def core_copy(way, c):
         return remote(
@@ -410,6 +430,11 @@
             to_chip.at[c], from_chip.at[c], send_chip.at[c], recv_chip.at[c], other_chip
         )
 
+    def store_copy(c):
+        return pltpu.make_async_copy(
+            result.at[c], out_ref.at[:, pl.ds(c * span, span)], store_sem.at[c]
+        )
+
     def project(way):
         for c in range(chunks):
             part = dot(flat[...], weight[:, c * span : (c + 1) * span])
@@ -417,21 +442,30 @@
             parts[way, c, 1] = part[quarter:]
             core_copy(way, c).start()
 
-    emit(1 - chip)
+    emit(1 - chip, mine)
+    for step in range(1, 8):
+        p = (place + 8 - step) % 8
+        head = ((p // 4 + upper) % 2) * 4 + p % 4
+        remote(
+            states.at[0], entering.at[head], send_down.at[0], recv_down.at[head], {"seq_1": mirror}
+        ).wait_recv()
+        emit(1 - chip, head)
     load.wait()
     project(0)
     for c in range(chunks):
         core_copy(0, c).wait_recv()
         to_chip[c] = parts[0, c, core] + from_core[0, c]
         chip_copy(c).start()
-    emit(chip)
+    for head in range(heads):
+        emit(chip, head)
     project(1)
     for c in range(chunks):
         core_copy(1, c).wait_recv()
     for c in range(chunks):
         chip_copy(c).wait_recv()
         total = parts[1, c, core] + from_core[1, c] + from_chip[c]
-        out_ref[:, c * span : (c + 1) * span] = total.astype(BF16)
+        result[c] = total.astype(BF16)
+        store_copy(c).start()
 
     for step in range(1, 8):
         p, target, head = peer(step)
@@ -445,13 +479,25 @@
 
     @pl.when((upper == 1) & (z < 3))
     def _():
-        for copy in chain:
-            copy.wait_send()
+        chain[2].wait_send()
+
+        @pl.when(z < 2)
+        def _():
+            chain[0].wait_send()
+
+        @pl.when(z == 1)
+        def _():
+            chain[1].wait_send()
+
+        @pl.when(z == 2)
+        def _():
+            lend.wait_send()
 
     for c in range(chunks):
         core_copy(0, c).wait_send()
         core_copy(1, c).wait_send()
         chip_copy(c).wait_send()
+        store_copy(c).wait()
 
 
 def body(queries, key_vecs, values, strength, decay_rate, norm_gain, w_out):
@@ -467,7 +513,7 @@
         layer_kernel,
         out_shape=jax.ShapeDtypeStruct((quarter, model), BF16),
         in_specs=[vmem] * 6 + [pl.BlockSpec(memory_space=pl.ANY)],
-        out_specs=vmem,
+        out_specs=pl.BlockSpec(memory_space=pl.ANY),
         scratch_shapes=[
             pltpu.VMEM((size * pairs, width), F32),
             pltpu.VMEM((size * pairs, width), F32),
@@ -482,6 +528,7 @@
             pltpu.VMEM((8, width, 2 * width), F32),
             pltpu.VMEM((width, 2 * width), F32),
             pltpu.VMEM((width, 2 * width), F32),
+            pltpu.VMEM((width, 2 * width), F32),
             pltpu.VMEM((8, width, width), F32),
             pltpu.VMEM((width, width), F32),
             pltpu.VMEM((width, width), F32),
@@ -492,17 +539,21 @@
             pltpu.VMEM((2, chunks, quarter, span), F32),
             pltpu.VMEM((chunks, quarter, span), F32),
             pltpu.VMEM((chunks, quarter, span), F32),
+            pltpu.VMEM((chunks, quarter, span), BF16),
             dma((8,)),
             dma((8,)),
             dma((2,)),
             dma((2,)),
-            dma((2,)),
+            dma((3,)),
+            dma,
+            dma,
             dma,
             dma((8,)),
             dma((8,)),
             dma,
             dma((2, chunks)),
             dma((2, chunks)),
+            dma((chunks,)),
             dma((chunks,)),
             dma((chunks,)),
         ],

time: 68.5 us -> 69.4 us (1.013)
  Pallas kernels: 66.7 us -> 67.6 us
    pallas_call x1, Pallas kernels: 66.7 us -> 67.6 us  [body(): pl.pallas_call(layer_kernel, out_shape=jax.ShapeDtypeStruct((quarter, mod...]
where the time goes in v5:
time: 69.4 us; the launch traced here: 69.2 us
  Pallas kernels  67.6 us (97%)
  local copies, waits for them, and re-layouts  1.67 us (2%)
    pallas_call x1, Pallas kernels, body(): pl.pallas_call(layer_kernel, out_shape=jax.ShapeDtypeStruct((quarter, mod...  67.6 us
    unnamed x1, local copies, waits for them, and re-layouts  1.67 us

profile of v5, /device:TPU:192, one launch (start us, length us, event | category | flops | bytes accessed | tf_op | source)
XLA Modules:
  0.0 69.2 jit_solution(13013795003311726558)
XLA Ops:
  0.0 67.6 %layer.1 = bf16[64,2048]{1,0:T(8,128)(2,1)} custom-call(bf16[1024,128]{1,0:T(8,128)(2,1)} %bitcast.7, bf16[1024,128]{1,0:T(8,128)(2,1)} %bitcast.8, bf16[2048,128]{1,0:T(8,128)(2,1)} %bitcast.6, f32[8,256]{1,0:T(8,128)} %bitcast.9, f32[8,256]{1,0:T(8,128)} %bitcast.10, f32[1,128]{1,0:T(1,128)} %bitcast.11, bf16[1024,2048]{1,0:T(8,128)(2,1)} %weight_hbm.1), custom_call_target="tpu_custom_call" | custom-call | tf_op jit(solution)/shard_map/layer/pallas_call | solution.py:512
  67.6 1.7 %copy.9 = bf16[64,2048]{1,0:T(8,128)(2,1)} copy(bf16[64,2048]{1,0:T(8,128)(2,1)} %layer.1) | data formatting | bytes 524288

commit v6 on v5

--- a/solution.py
+++ b/solution.py
@@ -313,6 +313,7 @@
         for i, (dz, at) in enumerate(((1, x), (2, x), (1, mirror)))
     ]
     lend = remote(plane, lent, send_lent, recv_lent, beside(1, x))
+    across = remote(passing, incoming, send_chain.at[0], recv_chain, {"seq_1": mirror})
 
     @pl.when(upper == 0)
     def _():
@@ -345,7 +346,7 @@
     def _():
         pair[1].wait_recv()
 
-    @pl.when((upper == 1) & (z > 0))
+    @pl.when((upper == 1) & (z > 0) & (z < 3))
     def _():
         plane[...] = then(prefix[7], lower_map[...])
 
@@ -364,22 +365,19 @@
     @pl.when((upper == 1) & (z == 3))
     def _():
         lend.wait_recv()
-        incoming[...] = (
+        passing[...] = (
             dot_split(split(lent[:, :width]), split(incoming[...])) + lent[:, width:]
         )
+        across.start()
+        incoming[...] = passing[...]
 
     before = split(incoming[...])
 
-    @pl.when((upper == 1) & (z > 0) & (z < 3))
+    @pl.when((upper == 1) & (z == 1))
     def _():
         passing[...] = dot_split(split(plane[:, :width]), before) + plane[:, width:]
-
-        @pl.when(z == 1)
-        def _():
-            chain[0].start()
-            chain[1].start()
-
-        chain[2].start()
+        for copy in (chain[1], chain[0], chain[2]):
+            copy.start()
 
     @pl.when(upper == 0)
     def _():
@@ -407,14 +405,17 @@
     quarter = size // 4
     chunks, _, span = to_chip.shape
 
-    def emit(side, head):
+    def emit(side):
         here = pl.ds(pl.multiple_of(side * half, half), half)
-        value = own_ref[head, here, :] + dot_split(
-            split(reach_ref[head, here, :]), split(entering[head])
-        )
-        mean = jnp.mean(value * value, axis=1, keepdims=True)
-        normed = value * lax.rsqrt(mean + norm_eps) * gain_ref[...]
-        flat[:, pl.ds(pl.multiple_of(head * width, width), width)] = normed.astype(BF16)
+        value = [
+            own_ref[head, here, :]
+            + dot_split(split(reach_ref[head, here, :]), split(entering[head]))
+            for head in range(heads)
+        ]
+        mean = [jnp.mean(x * x, axis=1, keepdims=True) for x in value]
+        for head in range(heads):
+            normed = value[head] * lax.rsqrt(mean[head] + norm_eps) * gain_ref[...]
+            flat[:, head * width : (head + 1) * width] = normed.astype(BF16)
 
     def core_copy(way, c):
         return remote(
@@ -442,22 +443,20 @@
             parts[way, c, 1] = part[quarter:]
             core_copy(way, c).start()
 
-    emit(1 - chip, mine)
     for step in range(1, 8):
         p = (place + 8 - step) % 8
         head = ((p // 4 + upper) % 2) * 4 + p % 4
         remote(
             states.at[0], entering.at[head], send_down.at[0], recv_down.at[head], {"seq_1": mirror}
         ).wait_recv()
-        emit(1 - chip, head)
+    emit(1 - chip)
     load.wait()
     project(0)
     for c in range(chunks):
         core_copy(0, c).wait_recv()
         to_chip[c] = parts[0, c, core] + from_core[0, c]
         chip_copy(c).start()
-    for head in range(heads):
-        emit(chip, head)
+    emit(chip)
     project(1)
     for c in range(chunks):
         core_copy(1, c).wait_recv()
@@ -477,21 +476,22 @@
         for copy in pair:
             copy.wait_send()
 
-    @pl.when((upper == 1) & (z < 3))
-    def _():
+    @pl.when((upper == 1) & (z < 2))
+    def _():
+        chain[0].wait_send()
         chain[2].wait_send()
 
-        @pl.when(z < 2)
-        def _():
-            chain[0].wait_send()
-
-        @pl.when(z == 1)
-        def _():
-            chain[1].wait_send()
-
-        @pl.when(z == 2)
-        def _():
-            lend.wait_send()
+    @pl.when((upper == 1) & (z == 1))
+    def _():
+        chain[1].wait_send()
+
+    @pl.when((upper == 1) & (z == 2))
+    def _():
+        lend.wait_send()
+
+    @pl.when((upper == 1) & (z == 3))
+    def _():
+        across.wait_send()
 
     for c in range(chunks):
         core_copy(0, c).wait_send()

time: 69.4 us -> 67.7 us (0.976)
  Pallas kernels: 67.6 us -> 65.9 us
    pallas_call x1, Pallas kernels: 67.6 us -> 65.9 us  [body(): pl.pallas_call(layer_kernel, out_shape=jax.ShapeDtypeStruct((quarter, mod...]
where the time goes in v6:
time: 67.7 us; the launch traced here: 67.6 us
  Pallas kernels  65.9 us (97%)
  local copies, waits for them, and re-layouts  1.67 us (2%)
    pallas_call x1, Pallas kernels, body(): pl.pallas_call(layer_kernel, out_shape=jax.ShapeDtypeStruct((quarter, mod...  65.9 us
    unnamed x1, local copies, waits for them, and re-layouts  1.67 us

profile of v6, /device:TPU:192, one launch (start us, length us, event | category | flops | bytes accessed | tf_op | source)
XLA Modules:
  0.0 67.6 jit_solution(11485889646222727037)
XLA Ops:
  0.0 65.9 %layer.1 = bf16[64,2048]{1,0:T(8,128)(2,1)} custom-call(bf16[1024,128]{1,0:T(8,128)(2,1)} %bitcast.7, bf16[1024,128]{1,0:T(8,128)(2,1)} %bitcast.8, bf16[2048,128]{1,0:T(8,128)(2,1)} %bitcast.6, f32[8,256]{1,0:T(8,128)} %bitcast.9, f32[8,256]{1,0:T(8,128)} %bitcast.10, f32[1,128]{1,0:T(1,128)} %bitcast.11, bf16[1024,2048]{1,0:T(8,128)(2,1)} %weight_hbm.1), custom_call_target="tpu_custom_call" | custom-call | tf_op jit(solution)/shard_map/layer/pallas_call | solution.py:512
  65.9 1.7 %copy.9 = bf16[64,2048]{1,0:T(8,128)(2,1)} copy(bf16[64,2048]{1,0:T(8,128)(2,1)} %layer.1) | data formatting | bytes 524288

commit v7 on v6

--- a/solution.py
+++ b/solution.py
@@ -308,12 +308,31 @@
         )
         for part in (1, 0)
     ]
-    chain = [
-        remote(passing, incoming, send_chain.at[i], recv_chain, beside(dz, at))
-        for i, (dz, at) in enumerate(((1, x), (2, x), (1, mirror)))
-    ]
+    def pass_on(n, target):
+        return [
+            remote(
+                passing.at[piece], incoming.at[piece], send_chain.at[n, i], recv_chain.at[i], target
+            )
+            for i, piece in enumerate(pieces)
+        ]
+
+    pieces = [pl.ds(i * (width // 2), width // 2) for i in range(2)]
+    to_next = pass_on(0, beside(1, x))
+    to_last = pass_on(1, beside(2, x))
+    to_next_lower = pass_on(2, beside(1, mirror))
+    across = pass_on(0, {"seq_1": mirror})
     lend = remote(plane, lent, send_lent, recv_lent, beside(1, x))
-    across = remote(passing, incoming, send_chain.at[0], recv_chain, {"seq_1": mirror})
+
+    def carry_over(total, copies):
+        through = split(total[:, :width])
+        offset = total[:, width:].T
+        for i, piece in enumerate(pieces):
+            to_next[i].wait_recv()
+            passing[piece, :] = (
+                dot_split(split(incoming[piece, :]), through, NT)
+                + offset[i * (width // 2) : (i + 1) * (width // 2), :]
+            )
+            copies[i].start()
 
     @pl.when(upper == 0)
     def _():
@@ -336,11 +355,11 @@
     @pl.when((upper == 1) & (z == 0))
     def _():
         passing[...] = (
-            dot_split(split(prefix[7, :, :width]), split(lower_map[:, width:]))
-            + prefix[7, :, width:]
-        )
-        chain[0].start()
-        chain[2].start()
+            dot_split(split(lower_map[:, width:].T), split(prefix[7, :, :width]), NT)
+            + prefix[7, :, width:].T
+        )
+        for copy in to_next + to_next_lower:
+            copy.start()
 
     @pl.when(upper == 1)
     def _():
@@ -358,34 +377,32 @@
     def _():
         incoming[...] = jnp.zeros_like(incoming)
 
-    @pl.when(z > 0)
-    def _():
-        chain[0].wait_recv()
+    @pl.when((z == 2) | ((upper == 0) & (z > 0)))
+    def _():
+        for copy in to_next:
+            copy.wait_recv()
+
+    @pl.when((upper == 1) & (z == 1))
+    def _():
+        carry_over(plane[...], to_last)
+        for copy in to_next_lower + to_next:
+            copy.start()
 
     @pl.when((upper == 1) & (z == 3))
     def _():
         lend.wait_recv()
-        passing[...] = (
-            dot_split(split(lent[:, :width]), split(incoming[...])) + lent[:, width:]
-        )
-        across.start()
+        carry_over(lent[...], across)
         incoming[...] = passing[...]
 
-    before = split(incoming[...])
-
-    @pl.when((upper == 1) & (z == 1))
-    def _():
-        passing[...] = dot_split(split(plane[:, :width]), before) + plane[:, width:]
-        for copy in (chain[1], chain[0], chain[2]):
-            copy.start()
-
     @pl.when(upper == 0)
     def _():
-        states[0] = incoming[...]
+        states[0] = incoming[...].T
 
     @pl.when(upper == 1)
     def _():
-        states[0] = dot_split(split(lower_map[:, :width]), before) + lower_map[:, width:]
+        states[0] = (
+            dot_split(split(lower_map[:, :width]), split(incoming[...]), NT) + lower_map[:, width:]
+        )
 
     ahead = split(states[0])
     for s in range(1, 8):
@@ -478,12 +495,13 @@
 
     @pl.when((upper == 1) & (z < 2))
     def _():
-        chain[0].wait_send()
-        chain[2].wait_send()
+        for copy in to_next + to_next_lower:
+            copy.wait_send()
 
     @pl.when((upper == 1) & (z == 1))
     def _():
-        chain[1].wait_send()
+        for copy in to_last:
+            copy.wait_send()
 
     @pl.when((upper == 1) & (z == 2))
     def _():
@@ -491,7 +509,8 @@
 
     @pl.when((upper == 1) & (z == 3))
     def _():
-        across.wait_send()
+        for copy in across:
+            copy.wait_send()
 
     for c in range(chunks):
         core_copy(0, c).wait_send()
@@ -544,8 +563,8 @@
             dma((8,)),
             dma((2,)),
             dma((2,)),
-            dma((3,)),
-            dma,
+            dma((3, 2)),
+            dma((2,)),
             dma,
             dma,
             dma((8,)),

time: 67.7 us -> 67 us (0.990)
  Pallas kernels: 65.9 us -> 65.2 us
where the time goes in v7:
time: 67 us; the launch traced here: 66.9 us
  Pallas kernels  65.2 us (97%)
  local copies, waits for them, and re-layouts  1.67 us (2%)
    pallas_call x1, Pallas kernels, body(): pl.pallas_call(layer_kernel, out_shape=jax.ShapeDtypeStruct((quarter, mod...  65.2 us
    unnamed x1, local copies, waits for them, and re-layouts  1.67 us

profile of v7, /device:TPU:192, one launch (start us, length us, event | category | flops | bytes accessed | tf_op | source)
XLA Modules:
  0.0 66.9 jit_solution(17584421352508416548)
XLA Ops:
  0.0 65.2 %layer.1 = bf16[64,2048]{1,0:T(8,128)(2,1)} custom-call(bf16[1024,128]{1,0:T(8,128)(2,1)} %bitcast.7, bf16[1024,128]{1,0:T(8,128)(2,1)} %bitcast.8, bf16[2048,128]{1,0:T(8,128)(2,1)} %bitcast.6, f32[8,256]{1,0:T(8,128)} %bitcast.9, f32[8,256]{1,0:T(8,128)} %bitcast.10, f32[1,128]{1,0:T(1,128)} %bitcast.11, bf16[1024,2048]{1,0:T(8,128)(2,1)} %weight_hbm.1), custom_call_target="tpu_custom_call" | custom-call | tf_op jit(solution)/shard_map/layer/pallas_call | solution.py:531
  65.3 1.7 %copy.9 = bf16[64,2048]{1,0:T(8,128)(2,1)} copy(bf16[64,2048]{1,0:T(8,128)(2,1)} %layer.1) | data formatting | bytes 524288

commit v8 on v7

--- a/solution.py
+++ b/solution.py
@@ -287,16 +287,14 @@
         moved = dot_split(split(later[:, :width]), split(running))
         return jnp.concatenate([moved[:, :width], moved[:, width:] + later[:, width:]], axis=1)
 
-    pairs_of = []
-    for s in range(0, 8, 2):
-        wait_map(s)
-        wait_map(s + 1)
-        pairs_of.append(then(arrived[s + 1], arrived[s]))
-    low_half = then(pairs_of[1], pairs_of[0])
-    high_half = then(pairs_of[3], pairs_of[2])
-    prefix[7] = then(high_half, low_half)
-    prefix[1] = pairs_of[0]
-    prefix[3] = low_half
+    for base in (side * 4, (1 - side) * 4):
+        for i in range(4):
+            wait_map(base + i)
+        early = then(arrived[base + 1], arrived[base])
+        late = then(arrived[base + 3], arrived[base + 2])
+        prefix[base + 1] = early
+        prefix[base + 3] = then(late, early)
+    prefix[7] = then(prefix[7], prefix[3])
 
     pair = [
         remote(
@@ -343,7 +341,7 @@
         prefix[0] = arrived[0]
         prefix[2] = then(arrived[2], prefix[1])
         prefix[4] = then(arrived[4], prefix[3])
-        prefix[5] = then(arrived[5], prefix[4])
+        prefix[5] = then(prefix[5], prefix[3])
         prefix[6] = then(arrived[6], prefix[5])
 
     rest_of_prefixes()

time: 67 us -> 67.6 us (level)
  no operation moved by 1% of the time
where the time goes in v8:
time: 67.6 us; the launch traced here: 67.5 us
  Pallas kernels  65.8 us (97%)
  local copies, waits for them, and re-layouts  1.67 us (2%)
    pallas_call x1, Pallas kernels, body(): pl.pallas_call(layer_kernel, out_shape=jax.ShapeDtypeStruct((quarter, mod...  65.8 us
    unnamed x1, local copies, waits for them, and re-layouts  1.67 us

profile of v8, /device:TPU:192, one launch (start us, length us, event | category | flops | bytes accessed | tf_op | source)
XLA Modules:
  0.0 67.5 jit_solution(14152553828136886152)
XLA Ops:
  0.0 65.8 %layer.1 = bf16[64,2048]{1,0:T(8,128)(2,1)} custom-call(bf16[1024,128]{1,0:T(8,128)(2,1)} %bitcast.7, bf16[1024,128]{1,0:T(8,128)(2,1)} %bitcast.8, bf16[2048,128]{1,0:T(8,128)(2,1)} %bitcast.6, f32[8,256]{1,0:T(8,128)} %bitcast.9, f32[8,256]{1,0:T(8,128)} %bitcast.10, f32[1,128]{1,0:T(1,128)} %bitcast.11, bf16[1024,2048]{1,0:T(8,128)(2,1)} %weight_hbm.1), custom_call_target="tpu_custom_call" | custom-call | tf_op jit(solution)/shard_map/layer/pallas_call | solution.py:529
  65.8 1.7 %copy.9 = bf16[64,2048]{1,0:T(8,128)(2,1)} copy(bf16[64,2048]{1,0:T(8,128)(2,1)} %layer.1) | data formatting | bytes 524288

commit v9 on v7

--- a/solution.py
+++ b/solution.py
@@ -182,7 +182,7 @@
         g_row, g_col, ratios = decay_ratios(rows, cols, head)
         mixing = split(jnp.where(row >= col, ratios * query_dots, 0.0))
         mixed = dot_split(mixing, split(solved_ref[head]))
-        reach_ref[head] = jnp.exp(g_col) * unit_q - mixed[:, :width]
+        reach_ref[0, head], reach_ref[1, head] = split(jnp.exp(g_col) * unit_q - mixed[:, :width])
         own_ref[head] = mixed[:, width:]
 
 
@@ -200,7 +200,7 @@
 def layer_kernel(
     q_ref, k_ref, v_ref, w_ref, d_ref, gain_ref, weight_hbm, out_ref,
     q32, k32, v32, rows, cols, maps_ref, solved_ref, own_ref, reach_ref,
-    arrived, prefix, lower_map, plane, lent, states, incoming, passing, entering,
+    arrived, prefix, through, lower_map, plane, lent, states, incoming, passing, entering,
     weight, flat, parts, from_core, to_chip, from_chip, result,
     send_maps, recv_maps, send_pair, recv_pair, send_chain, recv_chain, send_lent, recv_lent, send_down, recv_down,
     load_sem, send_core, recv_core, send_chip, recv_chip, store_sem,
@@ -324,12 +324,12 @@
     lend = remote(plane, lent, send_lent, recv_lent, beside(1, x))
 
     def carry_over(total, copies):
-        through = split(total[:, :width])
+        moving = split(total[:, :width])
         offset = total[:, width:].T
         for i, piece in enumerate(pieces):
             to_next[i].wait_recv()
             passing[piece, :] = (
-                dot_split(split(incoming[piece, :]), through, NT)
+                dot_split(split(incoming[piece, :]), moving, NT)
                 + offset[i * (width // 2) : (i + 1) * (width // 2), :]
             )
             copies[i].start()
@@ -347,6 +347,8 @@
         prefix[6] = then(arrived[6], prefix[5])
 
     rest_of_prefixes()
+    for s in range(7):
+        through[0, s], through[1, s] = split(prefix[s, :, :width])
 
     @pl.when(upper == 1)
     def _():
@@ -406,7 +408,9 @@
 
     ahead = split(states[0])
     for s in range(1, 8):
-        states[s] = dot_split(split(prefix[s - 1, :, :width]), ahead) + prefix[s - 1, :, width:]
+        states[s] = (
+            dot_split((through[0, s - 1], through[1, s - 1]), ahead) + prefix[s - 1, :, width:]
+        )
 
     def send_state(step):
         p, target, head = peer(step)
@@ -426,7 +430,9 @@
         here = pl.ds(pl.multiple_of(side * half, half), half)
         value = [
             own_ref[head, here, :]
-            + dot_split(split(reach_ref[head, here, :]), split(entering[head]))
+            + dot_split(
+                (reach_ref[0, head, here, :], reach_ref[1, head, here, :]), split(entering[head])
+            )
             for head in range(heads)
         ]
         mean = [jnp.mean(x * x, axis=1, keepdims=True) for x in value]
@@ -542,9 +548,10 @@
             pltpu.VMEM((heads, width, 2 * width), F32),
             pltpu.VMEM((heads, size, 2 * width), F32),
             pltpu.VMEM((heads, size, width), F32),
-            pltpu.VMEM((heads, size, width), F32),
+            pltpu.VMEM((2, heads, size, width), BF16),
             pltpu.VMEM((8, width, 2 * width), F32),
             pltpu.VMEM((8, width, 2 * width), F32),
+            pltpu.VMEM((2, 7, width, width), BF16),
             pltpu.VMEM((width, 2 * width), F32),
             pltpu.VMEM((width, 2 * width), F32),
             pltpu.VMEM((width, 2 * width), F32),

time: 67 us -> 67 us (level)
  no operation moved by 1% of the time
where the time goes in v9:
time: 67 us; the launch traced here: 66.9 us
  Pallas kernels  65.2 us (97%)
  local copies, waits for them, and re-layouts  1.67 us (2%)
    pallas_call x1, Pallas kernels, body(): pl.pallas_call(layer_kernel, out_shape=jax.ShapeDtypeStruct((quarter, mod...  65.2 us
    unnamed x1, local copies, waits for them, and re-layouts  1.67 us

profile of v9, /device:TPU:192, one launch (start us, length us, event | category | flops | bytes accessed | tf_op | source)
XLA Modules:
  0.0 66.9 jit_solution(7797668998319937079)
XLA Ops:
  0.0 65.2 %layer.1 = bf16[64,2048]{1,0:T(8,128)(2,1)} custom-call(bf16[1024,128]{1,0:T(8,128)(2,1)} %bitcast.7, bf16[1024,128]{1,0:T(8,128)(2,1)} %bitcast.8, bf16[2048,128]{1,0:T(8,128)(2,1)} %bitcast.6, f32[8,256]{1,0:T(8,128)} %bitcast.9, f32[8,256]{1,0:T(8,128)} %bitcast.10, f32[1,128]{1,0:T(1,128)} %bitcast.11, bf16[1024,2048]{1,0:T(8,128)(2,1)} %weight_hbm.1), custom_call_target="tpu_custom_call" | custom-call | tf_op jit(solution)/shard_map/layer/pallas_call | solution.py:537
  65.2 1.7 %copy.9 = bf16[64,2048]{1,0:T(8,128)(2,1)} copy(bf16[64,2048]{1,0:T(8,128)(2,1)} %layer.1) | data formatting | bytes 524288
